TPU v7x, 8 devices: a whole 2x2x1 slice. The times are simulated.
8 devices in a mesh: dp: 1 (over z), tp: 2 (over y), sp: 4 (over x, core).
Axes of the slice: x: 2, y: 2, z: 1, core: 2. Of those that a mesh axis runs over, the one named last changes fastest.
Arguments:
- tok_emb: bfloat16 [4, 32, 1536], P(None, 'dp')
- lengths: int32 [32], P('dp')
- key_cache: bfloat16 [2, 32, 4096, 2, 128], P(None, 'dp', 'sp', 'tp')
- val_cache: bfloat16 [2, 32, 4096, 2, 128], P(None, 'dp', 'sp', 'tp')
- gain_attn: bfloat16 [2, 1536], replicated
- gain_mlp: bfloat16 [2, 1536], replicated
- w_query: bfloat16 [2, 1536, 1536], P(None, None, 'tp')
- w_key: bfloat16 [2, 1536, 256], P(None, None, 'tp')
- w_value: bfloat16 [2, 1536, 256], P(None, None, 'tp')
- w_out: bfloat16 [2, 1536, 1536], P(None, 'tp')
- w_gate: bfloat16 [2, 1536, 8960], P(None, None, 'tp')
- w_up: bfloat16 [2, 1536, 8960], P(None, None, 'tp')
- w_down: bfloat16 [2, 8960, 1536], P(None, 'tp')
Outputs:
- output 1: bfloat16 [4, 32, 1536], P(None, 'dp')
- output 2: bfloat16 [2, 32, 4096, 2, 128], P(None, 'dp', 'sp', 'tp')
- output 3: bfloat16 [2, 32, 4096, 2, 128], P(None, 'dp', 'sp', 'tp')
All inputs are finite; a program needn't handle non-finite values.
Results may differ from a plain program's by a relative error of at most 0.0148625.
Values sent between devices are 32-bit elements.
A program may use at most 1 GiB of HBM per device.

v0:
```python
import jax
import jax.numpy as jnp
from jax import lax
from jax.sharding import PartitionSpec as P

EPS = 1e-5
ROPE_BASE = 500000.0


def rms_norm(hidden, gain_vec):
    x_float = hidden.astype(jnp.float32)
    inv_rms = lax.rsqrt(jnp.mean(x_float * x_float, axis=-1, keepdims=True) + EPS)
    return (x_float * inv_rms * gain_vec.astype(jnp.float32)).astype(jnp.bfloat16)


def rotary(in_vecs, positions):
    head_dim = in_vecs.shape[-1]
    half_dim = head_dim // 2
    inv_freq = 1.0 / (ROPE_BASE ** (jnp.arange(half_dim).astype(jnp.float32) * 2.0 / head_dim))
    angles = positions.astype(jnp.float32)[:, None] * inv_freq[None, :]
    cos_a = jnp.cos(angles)[:, None, :]
    sin_a = jnp.sin(angles)[:, None, :]
    front_half = in_vecs[..., :half_dim]
    back_half = in_vecs[..., half_dim:]
    return jnp.concatenate([front_half * cos_a - back_half * sin_a, back_half * cos_a + front_half * sin_a], axis=-1)


def project(normed, weight):
    return jnp.dot(normed, weight, preferred_element_type=jnp.float32)


def solution(mesh):
    sp_size = mesh.shape['sp']

    def local_fn(tok_emb, lengths, key_cache, val_cache, gain_attn, gain_mlp, w_query, w_key, w_value, w_out, w_gate, w_up, w_down):
        n_steps, n_batch, _ = tok_emb.shape
        n_layers, _, loc_len, kv_loc, head_dim = key_cache.shape
        heads_loc = w_query.shape[2] // head_dim
        group_size = heads_loc // kv_loc
        my_sp = lax.axis_index('sp')
        slot_pos = jnp.arange(loc_len) * sp_size + my_sp
        row_ids = jnp.arange(n_batch)
        new_keys = key_cache
        new_vals = val_cache
        hidden_list = []
        for step_idx in range(n_steps):
            cur_pos = lengths + step_idx
            write_slot = jnp.where(cur_pos % sp_size == my_sp, cur_pos // sp_size, loc_len)
            valid_mask = (slot_pos[None, :] <= cur_pos[:, None])[:, None, None, :]
            hidden = tok_emb[step_idx]
            for layer_idx in range(n_layers):
                normed = rms_norm(hidden, gain_attn[layer_idx])
                q_vec = project(normed, w_query[layer_idx]).reshape(n_batch, heads_loc, head_dim)
                k_vec = project(normed, w_key[layer_idx]).reshape(n_batch, kv_loc, head_dim)
                v_vec = project(normed, w_value[layer_idx]).reshape(n_batch, kv_loc, head_dim).astype(jnp.bfloat16)
                q_rot = rotary(q_vec, cur_pos).astype(jnp.bfloat16).reshape(n_batch, kv_loc, group_size, head_dim)
                k_rot = rotary(k_vec, cur_pos).astype(jnp.bfloat16)
                new_keys = new_keys.at[layer_idx, row_ids, write_slot].set(k_rot, mode='drop')
                new_vals = new_vals.at[layer_idx, row_ids, write_slot].set(v_vec, mode='drop')
                scores = jnp.einsum('bkgd,bjkd->bkgj', q_rot, new_keys[layer_idx], preferred_element_type=jnp.float32) * head_dim ** -0.5
                scores = jnp.where(valid_mask, scores, -1e30)
                loc_max = jnp.max(scores, axis=-1, keepdims=True)
                prob_w = jnp.exp(scores - loc_max)
                loc_sum = jnp.sum(prob_w, axis=-1, keepdims=True)
                loc_out = jnp.einsum('bkgj,bjkd->bkgd', prob_w.astype(jnp.bfloat16), new_vals[layer_idx], preferred_element_type=jnp.float32)
                glob_max = lax.pmax(loc_max, 'sp')
                rescale = jnp.exp(loc_max - glob_max)
                merged = lax.psum(jnp.concatenate([loc_out, loc_sum], axis=-1) * rescale, 'sp')
                attn_out = (merged[..., :head_dim] / merged[..., head_dim:]).astype(jnp.bfloat16).reshape(n_batch, heads_loc * head_dim)
                proj_sum = lax.psum(project(attn_out, w_out[layer_idx]), 'tp')
                hidden = (hidden.astype(jnp.float32) + proj_sum).astype(jnp.bfloat16)
                normed = rms_norm(hidden, gain_mlp[layer_idx])
                mlp_act = (jax.nn.silu(project(normed, w_gate[layer_idx])) * project(normed, w_up[layer_idx])).astype(jnp.bfloat16)
                down_sum = lax.psum(project(mlp_act, w_down[layer_idx]), 'tp')
                hidden = (hidden.astype(jnp.float32) + down_sum).astype(jnp.bfloat16)
            hidden_list.append(hidden)
        return jnp.stack(hidden_list), new_keys, new_vals

    cache_spec = P(None, 'dp', 'sp', 'tp', None)
    col_spec = P(None, None, 'tp')
    row_spec = P(None, 'tp', None)
    emb_spec = P(None, 'dp', None)
    return jax.shard_map(local_fn, mesh=mesh, in_specs=(emb_spec, P('dp'), cache_spec, cache_spec, P(), P(), col_spec, col_spec, col_spec, row_spec, col_spec, col_spec, row_spec), out_specs=(emb_spec, cache_spec, cache_spec), check_vma=False)
```

profile of v0, /device:TPU:0, one launch (start us, length us, event | category | flops | bytes accessed | tf_op | source)
XLA Modules:
  0.0 874.4 jit_solution(14325065001821498745)
XLA Ops:
  7.2 14.7 %copy.246 = bf16[2,32,1024,1,128]{4,2,3,1,0:T(8,128)(2,1)} copy(bf16[2,32,1024,1,128]{4,2,3,1,0:T(8,128)(2,1)} %param.15) | data formatting | bytes 33554432
  24.1 6.2 copy.247
  49.9 5.8 fusion.584
  55.7 13.1 %pmax.56 = f32[32,1,6,1]{2,0,3,1:T(8,128)S(1)} all-reduce(f32[32,1,6,1]{2,0,3,1:T(8,128)S(1)} %bitcast.610), channel_id=1, replica_groups=mesh['dp'=1,'tp'=2,'sp'=4] {'sp'}, use_global_device_ids=true, to_apply=%region_5.6 | all-reduce | flops 192 | bytes 1536 | tf_op jit(solution)/shard_map/pmax | solution.py:66
  93.9 13.9 %all-reduce.20.cloned.1.call-done = f32[32,1,6,129]{3,2,0,1:T(8,128)} async-done(((f32[32,1,6,129]{3,2,0,1:T(8,128)}), f32[32,1,6,129]{3,2,0,1:T(8,128)}) %all-reduce.20.cloned.1.call-update) | async-done | bytes 99088 | tf_op jit(solution)/shard_map/psum | solution.py:68
  115.0 14.7 %all-reduce.22.cloned.1.call-done = f32[32,1536]{1,0:T(8,128)} async-done(((f32[32,1536]{1,0:T(8,128)}), f32[32,1536]{1,0:T(8,128)}) %all-reduce.22.cloned.1.call-update) | async-done | bytes 196624 | tf_op jit(solution)/shard_map/psum | solution.py:70
  130.8 7.1 fusion.46
  137.9 12.3 %fusion.30 = f32[32,1536]{1,0:T(8,128)} fusion(bf16[2,4480,1536]{2,1,0:T(8,128)(2,1)} %param.25, bf16[2,1536,4480]{2,1,0:T(8,128)(2,1)} %param.24, f32[32,4480]{1,0:T(8,128)} %fusion.46, bf16[32,1536]{1,0:T(8,128)(2,1)S(1)} %get-tuple-element.59, f32[1536]{0:T(1024)S(1)} %get-tuple-element.17, f32[32]{0:T(128)S(1)} %add_rsqrt_fusion.14), kind=kOutput, calls=%fused_computation.46 | convolution fusion | flops 881860608 | bytes 28399744 | tf_op jit(solution)/shard_map/dot_general | solution.py:29
  151.0 16.0 %all-reduce.24.cloned.1.call-done = f32[32,1536]{1,0:T(8,128)} async-done(((f32[32,1536]{1,0:T(8,128)}), f32[32,1536]{1,0:T(8,128)}) %all-reduce.24.cloned.1.call-update) | async-done | bytes 196624 | tf_op jit(solution)/shard_map/psum | solution.py:74
  180.6 6.3 fusion.591
  191.5 6.7 fusion.585
  198.2 11.5 %pmax.58 = f32[32,1,6,1]{2,0,3,1:T(8,128)} all-reduce(f32[32,1,6,1]{2,0,3,1:T(8,128)S(1)} %bitcast.611), channel_id=1, replica_groups=mesh['dp'=1,'tp'=2,'sp'=4] {'sp'}, use_global_device_ids=true, to_apply=%region_25.26 | all-reduce | flops 192 | bytes 1536 | tf_op jit(solution)/shard_map/pmax | solution.py:66
  234.1 24.3 %all-reduce.26.cloned.1.call-done = f32[32,1,6,129]{3,2,0,1:T(8,128)} async-done(((f32[32,1,6,129]{3,2,0,1:T(8,128)}), f32[32,1,6,129]{3,2,0,1:T(8,128)}) %all-reduce.26.cloned.1.call-update) | async-done | bytes 99088 | tf_op jit(solution)/shard_map/psum | solution.py:68
  268.5 13.3 %all-reduce.28.cloned.1.call-done = f32[32,1536]{1,0:T(8,128)} async-done(((f32[32,1536]{1,0:T(8,128)}), f32[32,1536]{1,0:T(8,128)}) %all-reduce.28.cloned.1.call-update) | async-done | bytes 196624 | tf_op jit(solution)/shard_map/psum | solution.py:70
  283.6 7.1 fusion.44
  290.7 12.4 %fusion.28 = f32[32,1536]{1,0:T(8,128)} fusion(bf16[2,4480,1536]{2,1,0:T(8,128)(2,1)} %param.25, bf16[2,1536,4480]{2,1,0:T(8,128)(2,1)} %param.24, f32[32,4480]{1,0:T(8,128)} %fusion.44, bf16[32,1536]{1,0:T(8,128)(2,1)} %copy-done.18, f32[32]{0:T(128)S(1)} %add_rsqrt_fusion.10, f32[1536]{0:T(1024)} %copy-done.43), kind=kOutput, calls=%fused_computation.44 | convolution fusion | flops 881860608 | bytes 28401792 | tf_op jit(solution)/shard_map/dot_general | solution.py:29
  305.5 14.5 %all-reduce.30.cloned.1.call-done = f32[32,1536]{1,0:T(8,128)} async-done(((f32[32,1536]{1,0:T(8,128)}), f32[32,1536]{1,0:T(8,128)}) %all-reduce.30.cloned.1.call-update) | async-done | bytes 196624 | tf_op jit(solution)/shard_map/psum | solution.py:74
  338.3 7.3 fusion.590
  350.0 6.8 fusion.586
  356.8 10.9 %pmax.60 = f32[32,1,6,1]{2,0,3,1:T(8,128)} all-reduce(f32[32,1,6,1]{2,0,3,1:T(8,128)S(1)} %bitcast.612), channel_id=1, replica_groups=mesh['dp'=1,'tp'=2,'sp'=4] {'sp'}, use_global_device_ids=true, to_apply=%region_45.46 | all-reduce | flops 192 | bytes 1536 | tf_op jit(solution)/shard_map/pmax | solution.py:66
  371.1 5.6 fusion.179
  392.3 24.3 %all-reduce.32.cloned.1.call-done = f32[32,1,6,129]{3,2,0,1:T(8,128)} async-done(((f32[32,1,6,129]{3,2,0,1:T(8,128)}), f32[32,1,6,129]{3,2,0,1:T(8,128)}) %all-reduce.32.cloned.1.call-update) | async-done | bytes 99088 | tf_op jit(solution)/shard_map/psum | solution.py:68
  425.0 15.1 %all-reduce.34.cloned.1.call-done = f32[32,1536]{1,0:T(8,128)} async-done(((f32[32,1536]{1,0:T(8,128)}), f32[32,1536]{1,0:T(8,128)}) %all-reduce.34.cloned.1.call-update) | async-done | bytes 196624 | tf_op jit(solution)/shard_map/psum | solution.py:70
  441.2 7.1 fusion.42
  448.3 12.3 %fusion.26 = f32[32,1536]{1,0:T(8,128)} fusion(bf16[2,4480,1536]{2,1,0:T(8,128)(2,1)} %param.25, bf16[2,1536,4480]{2,1,0:T(8,128)(2,1)} %param.24, f32[32,4480]{1,0:T(8,128)} %fusion.42, bf16[32,1536]{1,0:T(8,128)(2,1)S(1)} %get-tuple-element.51, f32[32]{0:T(128)S(1)} %add_rsqrt_fusion.6, f32[1536]{0:T(1024)S(1)} %copy-done.44), kind=kOutput, calls=%fused_computation.42 | convolution fusion | flops 881860608 | bytes 28399744 | tf_op jit(solution)/shard_map/dot_general | solution.py:29
  463.6 13.8 %all-reduce.36.cloned.1.call-done = f32[32,1536]{1,0:T(8,128)} async-done(((f32[32,1536]{1,0:T(8,128)}), f32[32,1536]{1,0:T(8,128)}) %all-reduce.36.cloned.1.call-update) | async-done | bytes 196624 | tf_op jit(solution)/shard_map/psum | solution.py:74
  495.8 7.3 fusion.589
  507.4 6.7 fusion.587
  514.1 10.8 %pmax.62 = f32[32,1,6,1]{2,0,3,1:T(8,128)S(1)} all-reduce(f32[32,1,6,1]{2,0,3,1:T(8,128)S(1)} %bitcast.613), channel_id=1, replica_groups=mesh['dp'=1,'tp'=2,'sp'=4] {'sp'}, use_global_device_ids=true, to_apply=%region_65.66 | all-reduce | flops 192 | bytes 1536 | tf_op jit(solution)/shard_map/pmax | solution.py:66
  537.1 5.7 fusion.182
  546.2 26.7 %all-reduce.38.cloned.1.call-done = f32[32,1,6,129]{3,2,0,1:T(8,128)} async-done(((f32[32,1,6,129]{3,2,0,1:T(8,128)}), f32[32,1,6,129]{3,2,0,1:T(8,128)}) %all-reduce.38.cloned.1.call-update) | async-done | bytes 99088 | tf_op jit(solution)/shard_map/psum | solution.py:68
  583.6 13.4 %all-reduce.40.cloned.1.call-done = f32[32,1536]{1,0:T(8,128)} async-done(((f32[32,1536]{1,0:T(8,128)}), f32[32,1536]{1,0:T(8,128)}) %all-reduce.40.cloned.1.call-update) | async-done | bytes 196624 | tf_op jit(solution)/shard_map/psum | solution.py:70
  598.8 7.1 fusion.40
  605.9 12.4 %fusion.24 = f32[32,1536]{1,0:T(8,128)} fusion(bf16[2,4480,1536]{2,1,0:T(8,128)(2,1)} %param.25, bf16[2,1536,4480]{2,1,0:T(8,128)(2,1)} %param.24, f32[32,4480]{1,0:T(8,128)} %fusion.40, bf16[32,1536]{1,0:T(8,128)(2,1)} %copy-done.17, f32[32]{0:T(128)} %copy-done.55, f32[1536]{0:T(1024)} %copy-done.43), kind=kOutput, calls=%fused_computation.40 | convolution fusion | flops 881860608 | bytes 28402176 | tf_op jit(solution)/shard_map/dot_general | solution.py:29
  623.3 11.7 %all-reduce.42.cloned.1.call-done = f32[32,1536]{1,0:T(8,128)} async-done(((f32[32,1536]{1,0:T(8,128)}), f32[32,1536]{1,0:T(8,128)}) %all-reduce.42.cloned.1.call-update) | async-done | bytes 196624 | tf_op jit(solution)/shard_map/psum | solution.py:74
  650.1 5.7 fusion.588
  660.9 11.1 %all-reduce.1 = (f32[32,1,6,1]{2,0,3,1:T(8,128)S(1)}, f32[32,1,6,1]{2,0,3,1:T(8,128)S(1)}, f32[32,1,6,1]{2,0,3,1:T(8,128)S(1)}, f32[32,1,6,1]{2,0,3,1:T(8,128)S(1)}) all-reduce(f32[32,1,6,1]{2,0,3,1:T(8,128)S(1)} %bitcast.617, f32[32,1,6,1]{2,0,3,1:T(8,128)S(1)} %bitcast.616, ...), channel_id=1, replica_groups=mesh['dp'=1,'tp'=2,'sp'=4] {'sp'}, use_global_device_ids=true, to_apply=%region_75.76 | all-reduce | flops 768 | bytes 6144 | tf_op jit(solution)/shard_map/pmax | solution.py:66
  675.8 31.1 %all-reduce.44.cloned.1.call-done = (f32[32,1,6,129]{3,2,0,1:T(8,128)}, f32[32,1,6,129]{3,2,0,1:T(8,128)}, f32[32,1,6,129]{3,2,0,1:T(8,128)}, f32[32,1,6,129]{3,2,0,1:T(8,128)}) async-done(((f32[32,1,6,129]{3,2,0,1:T(8,128)}, f32[32,1,6,129]{3,2,0,1:T(8,128)}, f32[32,1,6,129]{3,2,0,1:T(8,128)}, f32[32,1,6,129]{3,2,0,1:T(8,128)}), (f32[32,1,6,129]{3,2,0,1:T(8,128)}, f32[32,1,6,129]{3,2,0,1:T(8,128)}, ...) | async-done | bytes 396304 | tf_op jit(solution)/shard_map/psum | solution.py:68
  727.4 28.7 %all-reduce.48.cloned.1.call-done = (f32[32,1536]{1,0:T(8,128)}, f32[32,1536]{1,0:T(8,128)}, f32[32,1536]{1,0:T(8,128)}, f32[32,1536]{1,0:T(8,128)}) async-done(((f32[32,1536]{1,0:T(8,128)}, f32[32,1536]{1,0:T(8,128)}, f32[32,1536]{1,0:T(8,128)}, f32[32,1536]{1,0:T(8,128)}), (f32[32,1536]{1,0:T(8,128)}, f32[32,1536]{1,0:T(8,128)}, f32[32,1536]{1,0:T(8,128)}, ...) | async-done | bytes 786448 | tf_op jit(solution)/shard_map/psum | solution.py:70
  760.5 6.3 fusion.22
  766.8 12.1 %fusion.6 = f32[32,1536]{1,0:T(8,128)} fusion(bf16[2,4480,1536]{2,1,0:T(8,128)(2,1)} %param.25, bf16[2,1536,4480]{2,1,0:T(8,128)(2,1)} %param.24, f32[32,4480]{1,0:T(8,128)S(1)} %fusion.22, bf16[32,1536]{1,0:T(8,128)(2,1)S(1)} %get-tuple-element.37, f32[1536]{0:T(1024)S(1)} %copy-done.42, f32[32]{0:T(128)S(1)} %add_rsqrt_fusion.12), kind=kOutput, calls=%fused_computation.22 | convolution fusion | flops 881860608 | bytes 28399744 | tf_op jit(solution)/shard_map/dot_general | solution.py:29
  779.0 6.3 fusion.20
  785.3 12.1 %fusion.4 = f32[32,1536]{1,0:T(8,128)} fusion(bf16[2,4480,1536]{2,1,0:T(8,128)(2,1)} %param.25, bf16[2,1536,4480]{2,1,0:T(8,128)(2,1)} %param.24, f32[32,4480]{1,0:T(8,128)S(1)} %fusion.20, bf16[32,1536]{1,0:T(8,128)(2,1)S(1)} %get-tuple-element.39, f32[32]{0:T(128)S(1)} %add_rsqrt_fusion.8, f32[1536]{0:T(1024)S(1)} %copy-done.42), kind=kOutput, calls=%fused_computation.20 | convolution fusion | flops 881860608 | bytes 28399744 | tf_op jit(solution)/shard_map/dot_general | solution.py:29
  797.4 6.3 fusion.18
  803.7 12.1 %fusion.2 = f32[32,1536]{1,0:T(8,128)} fusion(bf16[2,4480,1536]{2,1,0:T(8,128)(2,1)} %param.25, bf16[2,1536,4480]{2,1,0:T(8,128)(2,1)} %param.24, f32[32,4480]{1,0:T(8,128)S(1)} %fusion.18, bf16[32,1536]{1,0:T(8,128)(2,1)S(1)} %get-tuple-element.41, f32[32]{0:T(128)S(1)} %add_rsqrt_fusion.4, f32[1536]{0:T(1024)S(1)} %copy-done.42), kind=kOutput, calls=%fused_computation.18 | convolution fusion | flops 881860608 | bytes 28399744 | tf_op jit(solution)/shard_map/dot_general | solution.py:29
  815.8 6.3 fusion.16
  822.1 12.1 %fusion = f32[32,1536]{1,0:T(8,128)} fusion(bf16[2,4480,1536]{2,1,0:T(8,128)(2,1)} %param.25, bf16[2,1536,4480]{2,1,0:T(8,128)(2,1)} %param.24, f32[32,4480]{1,0:T(8,128)S(1)} %fusion.16, bf16[32,1536]{1,0:T(8,128)(2,1)S(1)} %get-tuple-element.43, f32[32]{0:T(128)S(1)} %add_rsqrt_fusion, f32[1536]{0:T(1024)S(1)} %copy-done.42), kind=kOutput, calls=%fused_computation.16 | convolution fusion | flops 881860608 | bytes 28399744 | tf_op jit(solution)/shard_map/dot_general | solution.py:29
  834.3 28.8 %all-reduce.46.cloned.1.call-done = (f32[32,1536]{1,0:T(8,128)}, f32[32,1536]{1,0:T(8,128)}, f32[32,1536]{1,0:T(8,128)}, f32[32,1536]{1,0:T(8,128)}) async-done(((f32[32,1536]{1,0:T(8,128)}, f32[32,1536]{1,0:T(8,128)}, f32[32,1536]{1,0:T(8,128)}, f32[32,1536]{1,0:T(8,128)}), (f32[32,1536]{1,0:T(8,128)}, f32[32,1536]{1,0:T(8,128)}, f32[32,1536]{1,0:T(8,128)}, ...) | async-done | bytes 786448 | tf_op jit(solution)/shard_map/psum | solution.py:74
  (325 shorter events, 275.3 us)
Async XLA Ops:
  7.2 100.6 %all-reduce.20.cloned.1.call-start = ((), (), s32[]{:S(2)}) async-start(), calls=%async_computation | async-start | bytes 524288 | tf_op jit(solution)/shard_map/psum | solution.py:68
  7.2 16.9 %copy-start = (bf16[2,32,1024,1,128]{4,2,3,1,0:T(8,128)(2,1)S(1)}, bf16[2,32,1024,1,128]{4,2,3,1,0:T(8,128)(2,1)}, u32[]{:S(2)}) copy-start(bf16[2,32,1024,1,128]{4,2,3,1,0:T(8,128)(2,1)} %param.16) | copy-start | bytes 50331652
  30.4 452.8 %copy-start.35 = (f32[64]{0:T(128)}, f32[64]{0:T(128)S(1)}, u32[]{:S(2)}) copy-start(f32[64]{0:T(128)S(1)} %negate_power_fusion) | copy-start | bytes 772
  30.4 13.2 %copy-start.37 = (f32[32]{0:T(128)}, f32[32]{0:T(128)S(1)}, u32[]{:S(2)}) copy-start(f32[32]{0:T(128)S(1)} %get-tuple-element.115) | copy-start | bytes 388
  30.4 13.2 %copy-start.38 = (f32[32]{0:T(128)}, f32[32]{0:T(128)S(1)}, u32[]{:S(2)}) copy-start(f32[32]{0:T(128)S(1)} %get-tuple-element.113) | copy-start | bytes 388
  31.3 81.8 %copy-start.24 = (f32[1536]{0:T(1024)}, f32[1536]{0:T(1024)S(1)}, u32[]{:S(2)}) copy-start(f32[1536]{0:T(1024)S(1)} %get-tuple-element.19) | copy-start | bytes 18436
  31.3 148.3 %copy-start.21 = (f32[1536]{0:T(1024)}, f32[1536]{0:T(1024)S(1)}, u32[]{:S(2)}) copy-start(f32[1536]{0:T(1024)S(1)} %get-tuple-element.18) | copy-start | bytes 18436
  44.1 36.9 %copy-start.50 = (f32[32]{0:T(128)S(1)}, f32[32]{0:T(128)}, u32[]{:S(2)}) copy-start(f32[32]{0:T(128)} %copy-done.49) | copy-start | bytes 388
  79.1 34.0 %copy-start.3 = (bf16[4,32,1536]{2,1,0:T(8,128)(2,1)S(1)}, bf16[4,32,1536]{2,1,0:T(8,128)(2,1)}, u32[]{:S(2)}) copy-start(bf16[4,32,1536]{2,1,0:T(8,128)(2,1)} %param.13) | copy-start | bytes 1179652
  80.9 48.8 %all-reduce.22.cloned.1.call-start = ((), (), s32[]{:S(2)}) async-start(), calls=%async_computation.1 | async-start | bytes 393216 | tf_op jit(solution)/shard_map/psum | solution.py:70
  84.7 53.1 %copy-start.43 = (f32[1536]{0:T(1024)}, f32[1536]{0:T(1024)S(1)}, u32[]{:S(2)}) copy-start(f32[1536]{0:T(1024)S(1)} %get-tuple-element.17) | copy-start | bytes 18436
  112.9 54.1 %all-reduce.24.cloned.1.call-start = ((), (), s32[]{:S(2)}) async-start(), calls=%async_computation.2 | async-start | bytes 393216 | tf_op jit(solution)/shard_map/psum | solution.py:74
  137.9 32.8 %copy-start.41 = (f32[32]{0:T(128)S(1)}, f32[32]{0:T(128)}, u32[]{:S(2)}) copy-start(f32[32]{0:T(128)} %copy-done.40) | copy-start | bytes 388
  137.9 42.5 %copy-start.30 = (f32[32,64]{1,0:T(8,128)S(1)}, f32[32,64]{1,0:T(8,128)}, u32[]{:S(2)}) copy-start(f32[32,64]{1,0:T(8,128)} %copy-done.29) | copy-start | bytes 24580
  137.9 42.5 %copy-start.32 = (f32[32,64]{1,0:T(8,128)S(1)}, f32[32,64]{1,0:T(8,128)}, u32[]{:S(2)}) copy-start(f32[32,64]{1,0:T(8,128)} %copy-done.31) | copy-start | bytes 24580
  150.2 36.8 %copy-start.33 = (bf16[32,128]{1,0:T(8,128)(2,1)S(1)}, bf16[32,128]{1,0:T(8,128)(2,1)}, u32[]{:S(2)}) copy-start(bf16[32,128]{1,0:T(8,128)(2,1)} %maximum_bitcast_fusion.2) | copy-start | bytes 24580
  150.2 108.2 %all-reduce.26.cloned.1.call-start = ((), (), s32[]{:S(2)}) async-start(), calls=%async_computation.3 | async-start | bytes 524288 | tf_op jit(solution)/shard_map/psum | solution.py:68
  191.5 40.7 %copy-start.47 = (f32[32]{0:T(128)S(1)}, f32[32]{0:T(128)}, u32[]{:S(2)}) copy-start(f32[32]{0:T(128)} %get-tuple-element.149) | copy-start | bytes 388
  232.1 49.8 %all-reduce.28.cloned.1.call-start = ((), (), s32[]{:S(2)}) async-start(), calls=%async_computation.4 | async-start | bytes 393216 | tf_op jit(solution)/shard_map/psum | solution.py:70
  265.1 54.9 %all-reduce.30.cloned.1.call-start = ((), (), s32[]{:S(2)}) async-start(), calls=%async_computation.5 | async-start | bytes 393216 | tf_op jit(solution)/shard_map/psum | solution.py:74
  290.7 30.4 %copy-start.22 = (f32[1536]{0:T(1024)S(1)}, f32[1536]{0:T(1024)}, u32[]{:S(2)}) copy-start(f32[1536]{0:T(1024)} %copy-done.21) | copy-start | bytes 18436
  303.1 113.5 %all-reduce.32.cloned.1.call-start = ((), (), s32[]{:S(2)}) async-start(), calls=%async_computation.6 | async-start | bytes 524288 | tf_op jit(solution)/shard_map/psum | solution.py:68
  350.0 40.4 %copy-start.26 = (f32[1536]{0:T(1024)S(1)}, f32[1536]{0:T(1024)}, u32[]{:S(2)}) copy-start(f32[1536]{0:T(1024)} %copy-done.24) | copy-start | bytes 18436
  350.0 40.4 %copy-start.52 = (f32[32]{0:T(128)S(1)}, f32[32]{0:T(128)}, u32[]{:S(2)}) copy-start(f32[32]{0:T(128)} %copy-done.51) | copy-start | bytes 388
  386.8 61.5 %copy-start.44 = (f32[1536]{0:T(1024)S(1)}, f32[1536]{0:T(1024)}, u32[]{:S(2)}) copy-start(f32[1536]{0:T(1024)} %copy-done.43) | copy-start | bytes 18436
  390.3 49.8 %all-reduce.34.cloned.1.call-start = ((), (), s32[]{:S(2)}) async-start(), calls=%async_computation.7 | async-start | bytes 393216 | tf_op jit(solution)/shard_map/psum | solution.py:70
  423.3 54.1 %all-reduce.36.cloned.1.call-start = ((), (), s32[]{:S(2)}) async-start(), calls=%async_computation.8 | async-start | bytes 393216 | tf_op jit(solution)/shard_map/psum | solution.py:74
  460.6 46.8 %copy-start.19 = (pred[32,1024]{1,0:T(8,128)(4,1)S(1)}, pred[32,1024]{1,0:T(8,128)(4,1)}, u32[]{:S(2)}) copy-start(pred[32,1024]{1,0:T(8,128)(4,1)} %get-tuple-element.94) | copy-start | bytes 98308
  460.6 112.3 %all-reduce.38.cloned.1.call-start = ((), (), s32[]{:S(2)}) async-start(), calls=%async_computation.9 | async-start | bytes 524288 | tf_op jit(solution)/shard_map/psum | solution.py:68
  514.1 13.5 %copy-start.13 = (f32[32,6]{1,0:T(8,128)}, f32[32,6]{1,0:T(8,128)S(1)}, u32[]{:S(2)}) copy-start(f32[32,6]{1,0:T(8,128)S(1)} %get-tuple-element.139) | copy-start | bytes 2308
  514.1 84.6 %copy-start.45 = (f32[1536]{0:T(1024)S(1)}, f32[1536]{0:T(1024)}, u32[]{:S(2)}) copy-start(f32[1536]{0:T(1024)} %copy-done.43) | copy-start | bytes 18436
  546.2 50.8 %all-reduce.40.cloned.1.call-start = ((), (), s32[]{:S(2)}) async-start(), calls=%async_computation.10 | async-start | bytes 393216 | tf_op jit(solution)/shard_map/psum | solution.py:70
  580.2 54.9 %all-reduce.42.cloned.1.call-start = ((), (), s32[]{:S(2)}) async-start(), calls=%async_computation.11 | async-start | bytes 393216 | tf_op jit(solution)/shard_map/psum | solution.py:74
  605.8 30.4 %copy-start.23 = (f32[1536]{0:T(1024)S(1)}, f32[1536]{0:T(1024)}, u32[]{:S(2)}) copy-start(f32[1536]{0:T(1024)} %copy-done.21) | copy-start | bytes 18436
  605.9 34.5 %copy-start.36 = (f32[64]{0:T(128)S(1)}, f32[64]{0:T(128)}, u32[]{:S(2)}) copy-start(f32[64]{0:T(128)} %copy-done.35) | copy-start | bytes 772
  618.3 88.5 %all-reduce.44.cloned.1.call-start = ((), (), s32[]{:S(2)}) async-start(), calls=%async_computation.12 | async-start | bytes 2097152 | tf_op jit(solution)/shard_map/psum | solution.py:68
  620.4 40.5 %copy-start.14 = (f32[32,6]{1,0:T(8,128)S(1)}, f32[32,6]{1,0:T(8,128)}, u32[]{:S(2)}) copy-start(f32[32,6]{1,0:T(8,128)} %get-tuple-element.147) | copy-start | bytes 2308
  620.4 40.5 %copy-start.15 = (f32[32,6]{1,0:T(8,128)S(1)}, f32[32,6]{1,0:T(8,128)}, u32[]{:S(2)}) copy-start(f32[32,6]{1,0:T(8,128)} %get-tuple-element.145) | copy-start | bytes 2308
  620.4 40.5 %copy-start.16 = (f32[32,6]{1,0:T(8,128)S(1)}, f32[32,6]{1,0:T(8,128)}, u32[]{:S(2)}) copy-start(f32[32,6]{1,0:T(8,128)} %get-tuple-element.143) | copy-start | bytes 2308
  620.4 52.1 %copy-start.10 = (f32[32,1,6,128]{3,2,0,1:T(8,128)S(1)}, f32[32,1,6,128]{3,2,0,1:T(8,128)}, u32[]{:S(2)}) copy-start(f32[32,1,6,128]{3,2,0,1:T(8,128)} %fusion.177) | copy-start | bytes 294916
  620.4 52.1 %copy-start.12 = (f32[32,1,6,1]{3,2,0,1:T(8,128)S(1)}, f32[32,1,6,1]{3,2,0,1:T(8,128)}, u32[]{:S(2)}) copy-start(f32[32,1,6,1]{3,2,0,1:T(8,128)} %copy.73) | copy-start | bytes 2308
  620.4 52.9 %copy-start.11 = (f32[32,1,6,128]{3,2,0,1:T(8,128)S(1)}, f32[32,1,6,128]{3,2,0,1:T(8,128)}, u32[]{:S(2)}) copy-start(f32[32,1,6,128]{3,2,0,1:T(8,128)} %fusion.179) | copy-start | bytes 294916
  656.2 101.0 %copy-start.9 = (bf16[32,1536]{1,0:T(8,128)(2,1)S(1)}, bf16[32,1536]{1,0:T(8,128)(2,1)}, u32[]{:S(2)}) copy-start(bf16[32,1536]{1,0:T(8,128)(2,1)} %copy-done.8) | copy-start | bytes 294916
  656.2 102.1 %copy-start.7 = (bf16[32,1536]{1,0:T(8,128)(2,1)S(1)}, bf16[32,1536]{1,0:T(8,128)(2,1)}, u32[]{:S(2)}) copy-start(bf16[32,1536]{1,0:T(8,128)(2,1)} %copy-done.6) | copy-start | bytes 294916
  656.2 103.2 %copy-start.5 = (bf16[32,1536]{1,0:T(8,128)(2,1)S(1)}, bf16[32,1536]{1,0:T(8,128)(2,1)}, u32[]{:S(2)}) copy-start(bf16[32,1536]{1,0:T(8,128)(2,1)} %copy-done.4) | copy-start | bytes 294916
  656.2 104.3 %copy-start.42 = (f32[1536]{0:T(1024)S(1)}, f32[1536]{0:T(1024)}, u32[]{:S(2)}) copy-start(f32[1536]{0:T(1024)} %get-tuple-element.16) | copy-start | bytes 18436
  675.7 80.5 %all-reduce.48.cloned.1.call-start = ((), (), s32[]{:S(2)}) async-start(), calls=%async_computation.14 | async-start | bytes 1572864 | tf_op jit(solution)/shard_map/psum | solution.py:70
  727.2 135.9 %all-reduce.46.cloned.1.call-start = ((), (), s32[]{:S(2)}) async-start(), calls=%async_computation.13 | async-start | bytes 1572864 | tf_op jit(solution)/shard_map/psum | solution.py:74
  (23 other events, 166.4 us)
Sparse Core Ops, SparseCore 0:
  81.0 26.7 all-reduce.19
  113.0 16.6 all-reduce.21
  150.3 16.6 all-reduce.23
  232.2 26.1 all-reduce.25
  265.2 16.6 all-reduce.27
  303.2 16.6 all-reduce.29
  390.4 26.1 all-reduce.31
  423.4 16.6 all-reduce.33
  460.7 16.6 all-reduce.35
  546.3 26.6 all-reduce.37
  580.3 16.6 all-reduce.39
  618.4 16.6 all-reduce.41
  675.8 30.9 all-reduce.43
  727.3 28.7 all-reduce.47
  834.4 28.5 all-reduce.45
where the time goes:
time: 886 us; the launch traced here: 874 us
  matrix products  301 us (34%)
  waiting for transfers between devices  291 us (33%)
  local copies, waits for them, and re-layouts  131 us (15%)
  other arithmetic  76.8 us (9%)
  blocking collectives  57.3 us (6%)
  between operations  15.1 us (2%)
    dot_general x48, matrix products, project(): return jnp.dot(normed, weight, preferred_element_type=jnp.float32)  207 us
    psum x5, waiting for transfers between devices, local_fn(): lax.psum(jnp.concatenate([loc_out, loc_sum], axis=-1) * rescale, 'sp')  120 us
    psum x5, waiting for transfers between devices, local_fn(): proj_sum = lax.psum(project(attn_out, w_out[layer_idx]), 'tp')  85.3 us
    psum x5, waiting for transfers between devices, local_fn(): down_sum = lax.psum(project(mlp_act, w_down[layer_idx]), 'tp')  84.8 us
    pmax x5, blocking collectives, local_fn(): glob_max = lax.pmax(loc_max, 'sp')  57.3 us
    dot_general x8, matrix products, local_fn(): jnp.einsum('bkgd,bjkd->bkgj', q_rot, new_keys[layer_idx], preferred_eleme...  52.6 us
    dot_general x8, matrix products, local_fn(): jnp.einsum('bkgj,bjkd->bkgd', prob_w.astype(jnp.bfloat16), new_vals[layer...  42.2 us
    scatter x8, local copies, waits for them, and re-layouts, local_fn(): new_vals.at[layer_idx, row_ids, write_slot].set(v_vec, mode='drop')  35.5 us
  transfers between devices with their start and end apart: 15, of which 15 were waited for; matrix products, arithmetic and copies ran while one was open for 4% of the time, Pallas kernels for 0%

commit v1 on v0

v1 whole, which is shorter than its diff:
```python
import functools
import jax
import jax.numpy as jnp
from jax import lax
from jax.experimental import pallas as pl
from jax.experimental.pallas import tpu as pltpu
from jax.sharding import PartitionSpec as P

EPS = 1e-5
ROPE_BASE = 500000.0
F32 = jnp.float32
BF16 = jnp.bfloat16


def rms_norm(x_float, gain_row):
    inv_rms = lax.rsqrt(jnp.mean(x_float * x_float, axis=-1, keepdims=True) + EPS)
    return (x_float * inv_rms * gain_row).astype(BF16)


def attn_kernel(layer, n_steps, n_heads, offs_ref, u_ref, gain_ref, cos_ref, sin_ref, wq_hbm, wk_hbm, wv_hbm, kc_hbm, vc_hbm, *rest):
    if layer > 0:
        rest = rest[2:]
    o_ref, st_ref, ko_hbm, vo_hbm, wq_buf, wk_buf, wv_buf, kbuf, vbuf, q_sc, kn_sc, vn_sc, w_sem, in_sem, out_sem = rest
    n_rows = u_ref.shape[0]
    n_slots, head_dim = kbuf.shape[1], kbuf.shape[2]
    n_seq = kbuf.shape[0]
    n_pairs = n_seq // 2
    pair_rows = 2 * n_steps

    w_copies = [pltpu.make_async_copy(src.at[layer], dst, w_sem.at[i]) for i, (src, dst) in enumerate(((wq_hbm, wq_buf), (wk_hbm, wk_buf), (wv_hbm, wv_buf)))]
    for cp in w_copies:
        cp.start()

    def in_copies(i):
        sl = pl.ds(2 * i, 2)
        return (pltpu.make_async_copy(kc_hbm.at[layer, sl], kbuf.at[sl], in_sem.at[0, i]),
                pltpu.make_async_copy(vc_hbm.at[layer, sl], vbuf.at[sl], in_sem.at[1, i]))

    def out_copies(i):
        sl = pl.ds(2 * i, 2)
        return (pltpu.make_async_copy(kbuf.at[sl], ko_hbm.at[layer, sl], out_sem.at[0, i]),
                pltpu.make_async_copy(vbuf.at[sl], vo_hbm.at[layer, sl], out_sem.at[1, i]))

    @pl.loop(0, n_pairs)
    def _(i):
        for cp in in_copies(i):
            cp.start()

    h = rms_norm(u_ref[...].astype(F32), gain_ref[...].astype(F32))
    cos_t = cos_ref[...]
    sin_t = sin_ref[...]

    def rope(x):
        return (x * cos_t + pltpu.roll(x, head_dim // 2, 1) * sin_t).astype(BF16).astype(F32)

    for cp in w_copies:
        cp.wait()
    q_all = jnp.dot(h, wq_buf[...], preferred_element_type=F32)
    for hd in range(n_heads):
        q_sc[hd] = rope(q_all[:, hd * head_dim:(hd + 1) * head_dim])
    kn_sc[...] = rope(jnp.dot(h, wk_buf[...], preferred_element_type=F32))
    vn_sc[...] = jnp.dot(h, wv_buf[...], preferred_element_type=F32).astype(BF16).astype(F32)

    m_rows = n_heads * pair_rows
    scale = head_dim ** -0.5

    def pair_body(i):
        for cp in in_copies(i):
            cp.wait()
        sub = lax.broadcasted_iota(jnp.int32, (m_rows, 1), 0) % pair_rows
        first = sub < n_steps
        q48 = jnp.concatenate([q_sc[hd, pl.ds(pair_rows * i, pair_rows), :] for hd in range(n_heads)], axis=0).astype(BF16)
        scs = []
        for e in range(2):
            b = 2 * i + e
            off = offs_ref[0, b]
            slot = offs_ref[1, b]
            row = offs_ref[2, b]
            base = pl.multiple_of((slot // 16) * 16, 16)
            hit = lax.broadcasted_iota(jnp.int32, (16, head_dim), 0) == slot - base
            for buf, new in ((kbuf, kn_sc), (vbuf, vn_sc)):
                tile = buf[b, pl.ds(base, 16), :].astype(F32)
                new_row = new[pl.ds(row, 1), :]
                buf[b, pl.ds(base, 16), :] = jnp.where(hit, jnp.broadcast_to(new_row, (16, head_dim)), tile).astype(BF16)
            scs.append(lax.dot_general(q48, kbuf[b], (((1,), (1,)), ((), ())), preferred_element_type=F32))
        lim = (jnp.where(first, offs_ref[0, 2 * i] + sub, offs_ref[0, 2 * i + 1] + sub - n_steps)) // 4
        s = jnp.where(jnp.broadcast_to(first, scs[0].shape), scs[0], scs[1]) * scale
        slot_id = lax.broadcasted_iota(jnp.int32, s.shape, 1)
        s = jnp.where(slot_id <= lim, s, -1e30)
        m = jnp.max(s, axis=-1, keepdims=True)
        p = jnp.exp(s - m)
        l = jnp.sum(p, axis=-1, keepdims=True)
        pb = p.astype(BF16)
        o0 = jnp.dot(pb, vbuf[2 * i], preferred_element_type=F32)
        o1 = jnp.dot(pb, vbuf[2 * i + 1], preferred_element_type=F32)
        o = jnp.where(jnp.broadcast_to(first, o0.shape), o0, o1)
        lane = lax.broadcasted_iota(jnp.int32, (pair_rows, head_dim), 1)
        st = jnp.zeros((pair_rows, head_dim), F32)
        for hd in range(n_heads):
            rs = slice(hd * pair_rows, (hd + 1) * pair_rows)
            o_ref[hd, pl.ds(pair_rows * i, pair_rows), :] = o[rs]
            st = jnp.where(lane == hd, m[rs], jnp.where(lane == hd + 8, l[rs], st))
        st_ref[pl.ds(pair_rows * i, pair_rows), :] = st
        for cp in out_copies(i):
            cp.start()

    @pl.loop(0, n_pairs // 2)
    def _(i):
        pair_body(2 * i)
        pair_body(2 * i + 1)

    @pl.loop(0, n_pairs)
    def _(i):
        for cp in out_copies(i):
            cp.wait()


def attention(layer, n_steps, offs, u, gain, cos_t, sin_t, w_query, w_key, w_value, kc, vc, prev):
    n_layers, n_seq, n_slots, head_dim = kc.shape
    n_rows, d_model = u.shape
    q_cols = w_query.shape[2]
    n_heads = q_cols // head_dim
    any_spec = pl.BlockSpec(memory_space=pl.ANY)
    vm = pl.BlockSpec(memory_space=pltpu.VMEM)
    ins = [offs, u, gain, cos_t, sin_t, w_query, w_key, w_value, kc, vc]
    in_specs = [pl.BlockSpec(memory_space=pltpu.SMEM), vm, vm, vm, vm] + [any_spec] * 5
    aliases = {}
    if layer > 0:
        ins += list(prev)
        in_specs += [any_spec] * 2
        aliases = {10: 2, 11: 3}
    cache_t = jax.ShapeDtypeStruct(kc.shape, kc.dtype)
    return pl.pallas_call(
        functools.partial(attn_kernel, layer, n_steps, n_heads),
        out_shape=[jax.ShapeDtypeStruct((n_heads, n_rows, head_dim), F32), jax.ShapeDtypeStruct((n_rows, head_dim), F32), cache_t, cache_t],
        in_specs=in_specs,
        out_specs=[vm, vm, any_spec, any_spec],
        scratch_shapes=[
            pltpu.VMEM((d_model, q_cols), BF16), pltpu.VMEM((d_model, head_dim), BF16), pltpu.VMEM((d_model, head_dim), BF16),
            pltpu.VMEM((n_seq, n_slots, head_dim), BF16), pltpu.VMEM((n_seq, n_slots, head_dim), BF16),
            pltpu.VMEM((n_heads, n_rows, head_dim), F32), pltpu.VMEM((n_rows, head_dim), F32), pltpu.VMEM((n_rows, head_dim), F32),
            pltpu.SemaphoreType.DMA((3,)), pltpu.SemaphoreType.DMA((2, n_seq // 2)), pltpu.SemaphoreType.DMA((2, n_seq // 2)),
        ],
        input_output_aliases=aliases,
        compiler_params=pltpu.CompilerParams(vmem_limit_bytes=40 * 1024 * 1024),
        name=f"attn{layer}",
    )(*ins)


def solution(mesh):
    sp_size = mesh.shape['sp']

    def local_fn(tok_emb, lengths, key_cache, val_cache, gain_attn, gain_mlp, w_query, w_key, w_value, w_out, w_gate, w_up, w_down):
        n_steps, n_batch, d_model = tok_emb.shape
        n_layers, _, loc_len, kv_loc, head_dim = key_cache.shape
        n_heads = w_query.shape[2] // head_dim
        n_rows = n_steps * n_batch
        my_sp = lax.axis_index('sp')
        kc = key_cache.reshape(n_layers, n_batch, loc_len, head_dim)
        vc = val_cache.reshape(n_layers, n_batch, loc_len, head_dim)
        own_step = (my_sp - lengths) % sp_size
        offs = jnp.stack([lengths - my_sp, (lengths + own_step) // sp_size, jnp.arange(n_batch, dtype=jnp.int32) * n_steps + own_step]).astype(jnp.int32)
        positions = (lengths[:, None] + jnp.arange(n_steps)[None, :]).reshape(n_rows)
        half_dim = head_dim // 2
        inv_freq = 1.0 / (ROPE_BASE ** (jnp.arange(half_dim).astype(F32) * 2.0 / head_dim))
        angles = positions.astype(F32)[:, None] * inv_freq[None, :]
        cos_a, sin_a = jnp.cos(angles), jnp.sin(angles)
        cos_t = jnp.concatenate([cos_a, cos_a], axis=-1)
        sin_t = jnp.concatenate([-sin_a, sin_a], axis=-1)
        u = tok_emb.transpose(1, 0, 2).reshape(n_rows, d_model)
        prev = None
        for layer in range(n_layers):
            o, st, ko, vo = attention(layer, n_steps, offs, u, gain_attn[layer][None], cos_t, sin_t, w_query, w_key, w_value, kc, vc, prev)
            prev = (ko, vo)
            loc_max = st[:, :n_heads].T[..., None]
            loc_sum = st[:, 8:8 + n_heads].T[..., None]
            glob_max = lax.pmax(loc_max, 'sp')
            merged = lax.psum(jnp.concatenate([o, loc_sum], axis=-1) * jnp.exp(loc_max - glob_max), 'sp')
            attn_out = (merged[..., :head_dim] / merged[..., head_dim:]).astype(BF16).transpose(1, 0, 2).reshape(n_rows, n_heads * head_dim)
            proj = lax.psum(jnp.dot(attn_out, w_out[layer], preferred_element_type=F32), 'tp')
            u = (u.astype(F32) + proj).astype(BF16)
            h2 = rms_norm(u.astype(F32), gain_mlp[layer].astype(F32))
            act = (jax.nn.silu(jnp.dot(h2, w_gate[layer], preferred_element_type=F32)) * jnp.dot(h2, w_up[layer], preferred_element_type=F32)).astype(BF16)
            down = lax.psum(jnp.dot(act, w_down[layer], preferred_element_type=F32), 'tp')
            u = (u.astype(F32) + down).astype(BF16)
        hidden = u.reshape(n_batch, n_steps, d_model).transpose(1, 0, 2)
        return hidden, prev[0].reshape(key_cache.shape), prev[1].reshape(val_cache.shape)

    cache_spec = P(None, 'dp', 'sp', 'tp', None)
    col_spec = P(None, None, 'tp')
    row_spec = P(None, 'tp', None)
    emb_spec = P(None, 'dp', None)
    return jax.shard_map(local_fn, mesh=mesh, in_specs=(emb_spec, P('dp'), cache_spec, cache_spec, P(), P(), col_spec, col_spec, col_spec, row_spec, col_spec, col_spec, row_spec), out_specs=(emb_spec, cache_spec, cache_spec), check_vma=False)
```

time: 886 us -> 316 us (0.36); the launches traced: 874 us -> 315 us
  matrix products: 301 us -> 48.5 us
  waiting for transfers between devices: 291 us -> 173 us
  local copies, waits for them, and re-layouts: 131 us -> 15.4 us
  other arithmetic: 76.8 us -> 11.6 us
  blocking collectives: 57.3 us -> 25.1 us
  Pallas kernels: 0 us -> 26.9 us
    dot_general x64 -> x6, matrix products: 301 us -> 48.5 us  [the longest x2 25.5 us: local_fn(): jnp.dot(act, w_down[layer], preferred_element_type=F32)]
    psum x15 -> x6, waiting for transfers between devices: 290 us -> 173 us  [the longest x2 58.6 us: local_fn(): lax.psum(jnp.concatenate([o, loc_sum], axis=-1) * jnp.exp(loc_max - glob_...]
    scatter x16 -> x0, local copies, waits for them, and re-layouts: 70.9 us -> none  [the longest x8 35.5 us: local_fn(): new_vals.at[layer_idx, row_ids, write_slot].set(v_vec, mode='drop')]
    pmax x5 -> x2, blocking collectives: 57.3 us -> 25.1 us  [local_fn(): glob_max = lax.pmax(loc_max, 'sp')]
    pallas_call x0 -> x2, Pallas kernels: none -> 26.9 us  [attention(): pl.pallas_call(functools.partial(attn_kernel, layer, n_steps, n_heads), o...]
    unnamed x114 -> x14, local copies, waits for them, and re-layouts: 25.6 us -> 6.94 us
    another operation x18 -> x3, other arithmetic: 15.4 us -> 0.69 us  [local_fn(): jnp.stack([lengths - my_sp, (lengths + own_step) // sp_size, jnp.arange(n...]
    mul x18 -> x5, other arithmetic: 15.1 us -> 2.25 us  [the longest x4 2.21 us: local_fn(): jnp.concatenate([o, loc_sum], axis=-1) * jnp.exp(loc_max - glob_max)]
  transfers between devices with their start and end apart: 15 -> 6, of which waited for: 15 -> 6; matrix products, arithmetic and copies ran while one was open for 4% -> 0% of each run, Pallas kernels for 0% -> 0%
where the time goes in v1:
time: 316 us; the launch traced here: 315 us
  waiting for transfers between devices  173 us (55%)
  matrix products  48.5 us (15%)
  Pallas kernels  26.9 us (9%)
  blocking collectives  25.1 us (8%)
  local copies, waits for them, and re-layouts  15.4 us (5%)
  between operations  14.3 us (5%)
  other arithmetic  11.6 us (4%)
    psum x2, waiting for transfers between devices, local_fn(): lax.psum(jnp.concatenate([o, loc_sum], axis=-1) * jnp.exp(loc_max - glob_...  58.6 us
    psum x2, waiting for transfers between devices, local_fn(): lax.psum(jnp.dot(act, w_down[layer], preferred_element_type=F32), 'tp')  57.4 us
    psum x2, waiting for transfers between devices, local_fn(): lax.psum(jnp.dot(attn_out, w_out[layer], preferred_element_type=F32), 'tp')  57.3 us
    pallas_call x2, Pallas kernels, attention(): pl.pallas_call(functools.partial(attn_kernel, layer, n_steps, n_heads), o...  26.9 us
    dot_general x2, matrix products, local_fn(): jnp.dot(act, w_down[layer], preferred_element_type=F32)  25.5 us
    pmax x2, blocking collectives, local_fn(): glob_max = lax.pmax(loc_max, 'sp')  25.1 us
    dot_general x2, matrix products, local_fn(): jnp.dot(h2, w_gate[layer], preferred_element_type=F32)  16.8 us
    unnamed x14, local copies, waits for them, and re-layouts  6.94 us
  transfers between devices with their start and end apart: 6, of which 6 were waited for; matrix products, arithmetic and copies ran while one was open for 0% of the time, Pallas kernels for 0%

profile of v1, /device:TPU:0, one launch (start us, length us, event | category | flops | bytes accessed | tf_op | source)
XLA Modules:
  0.0 315.3 jit_solution(1516310872299612889)
XLA Ops:
  7.2 0.7 add_convert_fusion.2
  8.0 0.7 fusion.60
  8.6 0.8 fusion.63
  9.4 0.1 convert_element_type.67
  9.5 1.3 copy.26
  10.8 0.1 reshape.69.u_ref
  10.9 0.3 fusion.58
  11.3 0.1 pad_maximum_fusion
  11.4 2.3 copy-done
  13.7 1.1 copy-done.2
  14.9 1.1 copy-done.4
  16.0 13.4 %attn0.1 = (f32[6,128,128]{2,1,0:T(8,128)S(1)}, f32[128,128]{1,0:T(8,128)S(1)}, bf16[2,32,1024,128]{3,2,1,0:T(8,128)(2,1)}, bf16[2,32,1024,128]{3,2,1,0:T(8,128)(2,1)}) custom-call(s32[3,32]{1,0:T(4,128)S(1)} %pad_add_fusion.offs_ref, bf16[128,1536]{1,0:T(8,128)(2,1)S(1)} %reshape.69.u_ref, bf16[1,1536]{1,0:T(2,128)(2,1)S(1)} %get-tuple-element.38.gain_ref, ...), custom_call_target="tpu_custom_call" | custom-call | tf_op jit(solution)/shard_map/attn0/pallas_call | solution.py:133
  29.4 0.1 slice_bitcast_fusion.2
  29.5 13.8 %pmax.14 = f32[6,128,1]{0,1,2:T(8,128)S(1)} all-reduce(f32[6,128,1]{0,1,2:T(8,128)S(1)} %get-tuple-element.35), channel_id=1, replica_groups=mesh['dp'=1,'tp'=2,'sp'=4] {'sp'}, use_global_device_ids=true, to_apply=%region_0.1 | all-reduce | flops 768 | bytes 6144 | tf_op jit(solution)/shard_map/pmax | solution.py:177
  43.4 0.1 copy.28
  43.4 1.1 copy.27
  44.6 1.1 maximum_multiply_fusion
  45.8 29.5 %all-reduce.7.cloned.1.call-done = f32[6,128,129]{2,1,0:T(8,128)} async-done(((f32[6,128,129]{2,1,0:T(8,128)}), f32[6,128,129]{2,1,0:T(8,128)}) %all-reduce.7.cloned.1.call-update) | async-done | bytes 396304 | tf_op jit(solution)/shard_map/psum | solution.py:178
  75.3 1.2 slice_reduce_fusion.1
  76.5 1.2 fusion.50
  77.6 0.2 copy.29
  77.8 3.1 fusion.32
  81.0 28.6 %all-reduce.9.cloned.1.call-done = f32[128,1536]{1,0:T(8,128)} async-done(((f32[128,1536]{1,0:T(8,128)}), f32[128,1536]{1,0:T(8,128)}) %all-reduce.9.cloned.1.call-update) | async-done | bytes 786448 | tf_op jit(solution)/shard_map/psum | solution.py:180
  109.6 1.3 fusion.36
  111.0 8.4 %fusion.10 = f32[128,4480]{1,0:T(8,128)} fusion(bf16[2,1536,4480]{2,1,0:T(8,128)(2,1)} %param.23, bf16[128,1536]{1,0:T(8,128)(2,1)S(1)} %get-tuple-element.30, f32[1536]{0:T(1024)S(1)} %get-tuple-element.26, f32[128]{0:T(128)S(1)} %add_rsqrt_fusion.1), kind=kOutput, calls=%fused_computation.10 | convolution fusion | flops 1762394112 | bytes 16456192 | tf_op jit(solution)/shard_map/dot_general | solution.py:183
  119.4 12.8 %fusion.6 = f32[128,1536]{1,0:T(8,128)} fusion(bf16[2,4480,1536]{2,1,0:T(8,128)(2,1)} %param.25, bf16[2,1536,4480]{2,1,0:T(8,128)(2,1)} %param.24, f32[128,4480]{1,0:T(8,128)} %fusion.10, bf16[128,1536]{1,0:T(8,128)(2,1)S(1)} %get-tuple-element.30, f32[1536]{0:T(1024)S(1)} %get-tuple-element.26, f32[128]{0:T(128)S(1)} %add_rsqrt_fusion.1), kind=kOutput, calls=%fused_computation.6 | convolution fusion | flops 3527442432 | bytes 31005184 | tf_op jit(solution)/shard_map/dot_general | solution.py:184
  132.3 28.7 %all-reduce.11.cloned.1.call-done = f32[128,1536]{1,0:T(8,128)} async-done(((f32[128,1536]{1,0:T(8,128)}), f32[128,1536]{1,0:T(8,128)}) %all-reduce.11.cloned.1.call-update) | async-done | bytes 786448 | tf_op jit(solution)/shard_map/psum | solution.py:184
  161.0 1.2 fusion.39.u_ref
  162.2 2.3 copy-done.1
  164.5 13.5 %attn1.1 = (f32[6,128,128]{2,1,0:T(8,128)S(1)}, f32[128,128]{1,0:T(8,128)S(1)}, bf16[2,32,1024,128]{3,2,1,0:T(8,128)(2,1)}, bf16[2,32,1024,128]{3,2,1,0:T(8,128)(2,1)}) custom-call(s32[3,32]{1,0:T(4,128)S(1)} %pad_add_fusion.offs_ref, bf16[128,1536]{1,0:T(8,128)(2,1)S(1)} %fusion.39.u_ref, ...), custom_call_target="tpu_custom_call", output_to_operand_aliasing={{2}: (10, {}), {3}: (11, {})} | custom-call | tf_op jit(solution)/shard_map/attn1/pallas_call | solution.py:133
  178.0 0.1 slice_bitcast_fusion
  178.1 11.3 %pmax.15 = f32[6,128,1]{0,1,2:T(8,128)S(1)} all-reduce(f32[6,128,1]{0,1,2:T(8,128)S(1)} %get-tuple-element.33), channel_id=1, replica_groups=mesh['dp'=1,'tp'=2,'sp'=4] {'sp'}, use_global_device_ids=true, to_apply=%region_5.6 | all-reduce | flops 768 | bytes 6144 | tf_op jit(solution)/shard_map/pmax | solution.py:177
  189.4 0.1 copy.31
  189.5 1.1 copy.30
  190.6 1.1 maximum_multiply_fusion.1
  191.8 29.1 %all-reduce.13.cloned.1.call-done = f32[6,128,129]{2,1,0:T(8,128)} async-done(((f32[6,128,129]{2,1,0:T(8,128)}), f32[6,128,129]{2,1,0:T(8,128)}) %all-reduce.13.cloned.1.call-update) | async-done | bytes 396304 | tf_op jit(solution)/shard_map/psum | solution.py:178
  220.8 1.2 slice_reduce_fusion
  222.0 1.2 fusion.51
  223.2 0.2 copy.32
  223.4 3.1 fusion.30
  226.5 28.7 %all-reduce.15.cloned.1.call-done = f32[128,1536]{1,0:T(8,128)} async-done(((f32[128,1536]{1,0:T(8,128)}), f32[128,1536]{1,0:T(8,128)}) %all-reduce.15.cloned.1.call-update) | async-done | bytes 786448 | tf_op jit(solution)/shard_map/psum | solution.py:180
  255.2 1.3 fusion.40
  256.5 8.4 %fusion.4 = f32[128,4480]{1,0:T(8,128)} fusion(bf16[2,1536,4480]{2,1,0:T(8,128)(2,1)} %param.23, bf16[128,1536]{1,0:T(8,128)(2,1)S(1)} %get-tuple-element.28, f32[1536]{0:T(1024)S(1)} %get-tuple-element.25, f32[128]{0:T(128)S(1)} %add_rsqrt_fusion), kind=kOutput, calls=%fused_computation.4 | convolution fusion | flops 1762394112 | bytes 16456192 | tf_op jit(solution)/shard_map/dot_general | solution.py:183
  264.9 12.7 %fusion = f32[128,1536]{1,0:T(8,128)} fusion(bf16[2,4480,1536]{2,1,0:T(8,128)(2,1)} %param.25, bf16[2,1536,4480]{2,1,0:T(8,128)(2,1)} %param.24, f32[128,4480]{1,0:T(8,128)} %fusion.4, bf16[128,1536]{1,0:T(8,128)(2,1)S(1)} %get-tuple-element.28, f32[1536]{0:T(1024)S(1)} %get-tuple-element.25, f32[128]{0:T(128)S(1)} %add_rsqrt_fusion), kind=kOutput, calls=%fused_computation | convolution fusion | flops 3527442432 | bytes 31005184 | tf_op jit(solution)/shard_map/dot_general | solution.py:184
  277.7 28.7 %all-reduce.17.cloned.1.call-done = f32[128,1536]{1,0:T(8,128)} async-done(((f32[128,1536]{1,0:T(8,128)}), f32[128,1536]{1,0:T(8,128)}) %all-reduce.17.cloned.1.call-update) | async-done | bytes 786448 | tf_op jit(solution)/shard_map/psum | solution.py:184
  306.4 1.2 fusion.43
  307.6 0.1 reshape.74
  307.7 0.8 copy.37
  (30 shorter events, 0.5 us)
Async XLA Ops:
  7.2 68.1 %all-reduce.7.cloned.1.call-start = ((), (), s32[]{:S(2)}) async-start(), calls=%async_computation | async-start | bytes 1572864 | tf_op jit(solution)/shard_map/psum | solution.py:178
  11.4 2.3 copy-start
  13.7 1.1 copy-start.2
  14.8 1.1 copy-start.4
  29.4 51.6 %copy-start.6 = (bf16[2,1536]{1,0:T(2,128)(2,1)S(1)}, bf16[2,1536]{1,0:T(2,128)(2,1)}, u32[]{:S(2)}) copy-start(bf16[2,1536]{1,0:T(2,128)(2,1)} %param.18) | copy-start | bytes 18436
  45.7 63.9 %all-reduce.9.cloned.1.call-start = ((), (), s32[]{:S(2)}) async-start(), calls=%async_computation.1 | async-start | bytes 1572864 | tf_op jit(solution)/shard_map/psum | solution.py:180
  80.9 80.0 %all-reduce.11.cloned.1.call-start = ((), (), s32[]{:S(2)}) async-start(), calls=%async_computation.2 | async-start | bytes 1572864 | tf_op jit(solution)/shard_map/psum | solution.py:184
  119.4 42.8 %copy-start.3 = (bf16[2,1536,128]{2,1,0:T(8,128)(2,1)S(1)}, bf16[2,1536,128]{2,1,0:T(8,128)(2,1)}, u32[]{:S(2)}) copy-start(bf16[2,1536,128]{2,1,0:T(8,128)(2,1)} %wk_hbm.3) | copy-start | bytes 2359300
  119.4 42.8 %copy-start.5 = (bf16[2,1536,128]{2,1,0:T(8,128)(2,1)S(1)}, bf16[2,1536,128]{2,1,0:T(8,128)(2,1)}, u32[]{:S(2)}) copy-start(bf16[2,1536,128]{2,1,0:T(8,128)(2,1)} %wv_hbm.3) | copy-start | bytes 2359300
  132.2 88.6 %all-reduce.13.cloned.1.call-start = ((), (), s32[]{:S(2)}) async-start(), calls=%async_computation.3 | async-start | bytes 1572864 | tf_op jit(solution)/shard_map/psum | solution.py:178
  162.2 2.3 copy-start.1
  191.7 63.5 %all-reduce.15.cloned.1.call-start = ((), (), s32[]{:S(2)}) async-start(), calls=%async_computation.4 | async-start | bytes 1572864 | tf_op jit(solution)/shard_map/psum | solution.py:180
  226.5 79.9 %all-reduce.17.cloned.1.call-start = ((), (), s32[]{:S(2)}) async-start(), calls=%async_computation.5 | async-start | bytes 1572864 | tf_op jit(solution)/shard_map/psum | solution.py:184
Sparse Core Ops, SparseCore 0:
  45.8 29.4 all-reduce.6
  81.1 28.5 all-reduce.8
  132.4 28.5 all-reduce.10
  191.8 28.9 all-reduce.12
  226.6 28.5 all-reduce.14
  277.8 28.5 all-reduce.16

commit v2 on v1

--- a/solution.py
+++ b/solution.py
@@ -10,6 +10,7 @@
 ROPE_BASE = 500000.0
 F32 = jnp.float32
 BF16 = jnp.bfloat16
+MESH = pl.DeviceIdType.MESH
 
 
 def rms_norm(x_float, gain_row):
@@ -20,7 +21,7 @@
 def attn_kernel(layer, n_steps, n_heads, offs_ref, u_ref, gain_ref, cos_ref, sin_ref, wq_hbm, wk_hbm, wv_hbm, kc_hbm, vc_hbm, *rest):
     if layer > 0:
         rest = rest[2:]
-    o_ref, st_ref, ko_hbm, vo_hbm, wq_buf, wk_buf, wv_buf, kbuf, vbuf, q_sc, kn_sc, vn_sc, w_sem, in_sem, out_sem = rest
+    o_ref, ko_hbm, vo_hbm, wq_buf, wk_buf, wv_buf, kbuf, vbuf, q_sc, kn_sc, vn_sc, w_sem, in_sem, out_sem = rest
     n_rows = u_ref.shape[0]
     n_slots, head_dim = kbuf.shape[1], kbuf.shape[2]
     n_seq = kbuf.shape[0]
@@ -100,7 +101,7 @@
             rs = slice(hd * pair_rows, (hd + 1) * pair_rows)
             o_ref[hd, pl.ds(pair_rows * i, pair_rows), :] = o[rs]
             st = jnp.where(lane == hd, m[rs], jnp.where(lane == hd + 8, l[rs], st))
-        st_ref[pl.ds(pair_rows * i, pair_rows), :] = st
+        o_ref[n_heads, pl.ds(pair_rows * i, pair_rows), :] = st
         for cp in out_copies(i):
             cp.start()
 
@@ -128,13 +129,13 @@
     if layer > 0:
         ins += list(prev)
         in_specs += [any_spec] * 2
-        aliases = {10: 2, 11: 3}
+        aliases = {10: 1, 11: 2}
     cache_t = jax.ShapeDtypeStruct(kc.shape, kc.dtype)
     return pl.pallas_call(
         functools.partial(attn_kernel, layer, n_steps, n_heads),
-        out_shape=[jax.ShapeDtypeStruct((n_heads, n_rows, head_dim), F32), jax.ShapeDtypeStruct((n_rows, head_dim), F32), cache_t, cache_t],
+        out_shape=[jax.ShapeDtypeStruct((n_heads + 1, n_rows, head_dim), F32), cache_t, cache_t],
         in_specs=in_specs,
-        out_specs=[vm, vm, any_spec, any_spec],
+        out_specs=[vm, any_spec, any_spec],
         scratch_shapes=[
             pltpu.VMEM((d_model, q_cols), BF16), pltpu.VMEM((d_model, head_dim), BF16), pltpu.VMEM((d_model, head_dim), BF16),
             pltpu.VMEM((n_seq, n_slots, head_dim), BF16), pltpu.VMEM((n_seq, n_slots, head_dim), BF16),
@@ -145,6 +146,173 @@
         compiler_params=pltpu.CompilerParams(vmem_limit_bytes=40 * 1024 * 1024),
         name=f"attn{layer}",
     )(*ins)
+
+
+def merge(a, b, n_heads):
+    lane = lax.broadcasted_iota(jnp.int32, a(n_heads).shape, 1)
+    st_a, st_b = a(n_heads), b(n_heads)
+    m = jnp.maximum(st_a, st_b)
+    fa, fb = jnp.exp(st_a - m), jnp.exp(st_b - m)
+    fa = jnp.where(lane < 8, fa, 0.0)
+    fb = jnp.where(lane < 8, fb, 0.0)
+    l = st_a * pltpu.roll(fa, 8, 1) + st_b * pltpu.roll(fb, 8, 1)
+    st = jnp.where(lane < 8, m, l)
+    outs = [a(hd) * fa[:, hd:hd + 1] + b(hd) * fb[:, hd:hd + 1] for hd in range(n_heads)]
+    return outs, st
+
+
+def mix_kernel(layer, n_heads, part_ref, u_ref, gain_ref, wo_hbm, wg_hbm, wu_hbm, wd_hbm, out_ref,
+               wo_buf, wg_buf, wu_buf, wd_buf, core_in, fwd_out, fwd_in, y_out, y_in, u1_sc, h_out, h_in, hh, act,
+               d_own, d_out, d_in, e_out, e_in, u_all, w_sem, send_sem, recv_sem):
+    tp = lax.axis_index('tp')
+    sp = lax.axis_index('sp')
+    core = lax.rem(sp, 2)
+    core_peer = {'sp': sp + 1 - 2 * core}
+    far_peer = {'sp': lax.rem(sp + 2, 4)}
+    tp_peer = {'tp': 1 - tp}
+    n_blk, chunk, width = y_out.shape
+    ff = wg_buf.shape[1]
+    skip = 2 * ff - wg_hbm.shape[2]
+    col0 = pl.multiple_of(core * (ff - skip), 128)
+
+    w_copies = [
+        pltpu.make_async_copy(wo_hbm.at[layer], wo_buf, w_sem.at[0]),
+        pltpu.make_async_copy(wg_hbm.at[layer, :, pl.ds(col0, ff)], wg_buf, w_sem.at[1]),
+        pltpu.make_async_copy(wu_hbm.at[layer, :, pl.ds(col0, ff)], wu_buf, w_sem.at[2]),
+        pltpu.make_async_copy(wd_hbm.at[layer, pl.ds(col0, ff), :], wd_buf, w_sem.at[3]),
+    ]
+    for cp in w_copies:
+        cp.start()
+
+    barrier = pltpu.get_barrier_semaphore()
+    for peer in (core_peer, far_peer, tp_peer):
+        pl.semaphore_signal(barrier, inc=1, device_id=peer, device_id_type=MESH)
+    pl.semaphore_wait(barrier, 3)
+
+    count = [0]
+
+    def remote(src, dst, peer):
+        k = count[0]
+        count[0] += 1
+        return pltpu.make_async_remote_copy(src_ref=src, dst_ref=dst, send_sem=send_sem.at[k], recv_sem=recv_sem.at[k], device_id=peer, device_id_type=MESH)
+
+    def rows(idx):
+        return pl.ds(pl.multiple_of(idx * chunk, chunk), chunk)
+
+    far_chunk = lax.rem(sp + 2, 4)
+    sib = sp + 1 - 2 * core
+    sib_far = lax.rem(sib + 2, 4)
+
+    c_far = remote(part_ref.at[:, rows(sib_far), :], core_in.at[0], core_peer)
+    c_own = remote(part_ref.at[:, rows(sib), :], core_in.at[1], core_peer)
+    c_far.start()
+    c_own.start()
+    fwd = remote(fwd_out, fwd_in, far_peer)
+    c_far.wait_recv()
+    outs, st = merge(lambda hd: part_ref[hd, rows(far_chunk), :], lambda hd: core_in[0, hd], n_heads)
+    for hd in range(n_heads):
+        fwd_out[hd] = outs[hd]
+    fwd_out[n_heads] = st
+    fwd.start()
+    c_own.wait_recv()
+    own, own_st = merge(lambda hd: part_ref[hd, rows(sp), :], lambda hd: core_in[1, hd], n_heads)
+    for hd in range(n_heads):
+        core_in[0, hd] = own[hd]
+    core_in[0, n_heads] = own_st
+    fwd.wait_recv()
+    outs, st = merge(lambda hd: core_in[0, hd], lambda hd: fwd_in[hd], n_heads)
+    attn_out = jnp.concatenate([(outs[hd] / st[:, 8 + hd:9 + hd]).astype(BF16) for hd in range(n_heads)], axis=1)
+
+    y_copies = [remote(y_out.at[n], y_in.at[n], tp_peer) for n in range(n_blk)]
+    w_copies[0].wait()
+    for n in range(n_blk):
+        y_out[n] = jnp.dot(attn_out, wo_buf[:, n * width:(n + 1) * width], preferred_element_type=F32)
+        y_copies[n].start()
+    for n in range(n_blk):
+        y_copies[n].wait_recv()
+        cols = slice(n * width, (n + 1) * width)
+        u1_sc[:, cols] = (u_ref[rows(sp), cols].astype(F32) + (y_out[n] + y_in[n])).astype(BF16).astype(F32)
+    h2 = rms_norm(u1_sc[...], gain_ref[...].astype(F32))
+    h_out[...] = h2.astype(F32)
+    hh[0:chunk, :] = h2
+    h_copy = remote(h_out, h_in, core_peer)
+    h_copy.start()
+    for cp in w_copies[1:]:
+        cp.wait()
+    h_copy.wait_recv()
+    hh[chunk:2 * chunk, :] = h_in[...].astype(BF16)
+
+    blk = 256
+    for n in range(ff // blk):
+        cols = slice(n * blk, (n + 1) * blk)
+        gate = jnp.dot(hh[...], wg_buf[:, cols], preferred_element_type=F32)
+        up = jnp.dot(hh[...], wu_buf[:, cols], preferred_element_type=F32)
+        val = gate / (1.0 + jnp.exp(-gate)) * up
+        if n * blk < skip:
+            lane = lax.broadcasted_iota(jnp.int32, val.shape, 1) + n * blk
+            val = jnp.where(lane < skip * core, 0.0, val)
+        act[:, cols] = val.astype(BF16)
+
+    d_copies = [remote(d_out.at[n], d_in.at[n], core_peer) for n in range(n_blk)]
+    e_copies = [remote(e_out.at[n], e_in.at[n], tp_peer) for n in range(n_blk)]
+    a_core = [remote(u_all.at[n, rows(sp), :], u_all.at[n, rows(sp), :], core_peer) for n in range(n_blk)]
+    a_far = [remote(u_all.at[n, rows(sp), :], u_all.at[n, rows(sp), :], far_peer) for n in range(n_blk)]
+    a_fwd = [remote(u_all.at[n, rows(far_chunk), :], u_all.at[n, rows(far_chunk), :], core_peer) for n in range(n_blk)]
+    for n in range(n_blk):
+        down = jnp.dot(act[...], wd_buf[:, n * width:(n + 1) * width], preferred_element_type=F32)
+        d_own[n] = down[:chunk]
+        d_out[n] = down[chunk:]
+        d_copies[n].start()
+    for n in range(n_blk):
+        d_copies[n].wait_recv()
+        e_out[n] = d_own[n] + d_in[n]
+        e_copies[n].start()
+    for n in range(n_blk):
+        e_copies[n].wait_recv()
+        u_all[n, rows(sp), :] = (u1_sc[:, n * width:(n + 1) * width] + (e_out[n] + e_in[n])).astype(BF16).astype(F32)
+        a_far[n].start()
+        a_core[n].start()
+    for n in range(n_blk):
+        a_far[n].wait_recv()
+        a_fwd[n].start()
+    for n in range(n_blk):
+        a_core[n].wait_recv()
+        a_fwd[n].wait_recv()
+        out_ref[:, n * width:(n + 1) * width] = u_all[n].astype(BF16)
+    for cp in [c_far, c_own, fwd, h_copy] + y_copies + d_copies + e_copies + a_core + a_far + a_fwd:
+        cp.wait_send()
+
+
+def mix(layer, part, u, gain, w_out, w_gate, w_up, w_down):
+    n_planes, n_rows, head_dim = part.shape
+    n_heads = n_planes - 1
+    d_model = u.shape[1]
+    chunk = n_rows // 4
+    n_tiles = w_gate.shape[2] // 128
+    ff = ((n_tiles + 1) // 2) * 128
+    n_blk = 3
+    width = d_model // n_blk
+    any_spec = pl.BlockSpec(memory_space=pl.ANY)
+    vm = pl.BlockSpec(memory_space=pltpu.VMEM)
+    blocks = pltpu.VMEM((n_blk, chunk, width), F32)
+    planes = pltpu.VMEM((n_planes, chunk, head_dim), F32)
+    n_copies = 4 + 6 * n_blk
+    return pl.pallas_call(
+        functools.partial(mix_kernel, layer, n_heads),
+        out_shape=jax.ShapeDtypeStruct((n_rows, d_model), BF16),
+        in_specs=[vm, vm, vm] + [any_spec] * 4,
+        out_specs=vm,
+        scratch_shapes=[
+            pltpu.VMEM((w_out.shape[1], d_model), BF16), pltpu.VMEM((d_model, ff), BF16), pltpu.VMEM((d_model, ff), BF16), pltpu.VMEM((ff, d_model), BF16),
+            pltpu.VMEM((2, n_planes, chunk, head_dim), F32), planes, planes,
+            blocks, blocks, pltpu.VMEM((chunk, d_model), F32), pltpu.VMEM((chunk, d_model), F32), pltpu.VMEM((chunk, d_model), F32),
+            pltpu.VMEM((2 * chunk, d_model), BF16), pltpu.VMEM((2 * chunk, ff), BF16),
+            blocks, blocks, blocks, blocks, blocks, pltpu.VMEM((n_blk, n_rows, width), F32),
+            pltpu.SemaphoreType.DMA((4,)), pltpu.SemaphoreType.DMA((n_copies,)), pltpu.SemaphoreType.DMA((n_copies,)),
+        ],
+        compiler_params=pltpu.CompilerParams(collective_id=layer, has_side_effects=True, vmem_limit_bytes=48 * 1024 * 1024),
+        name=f"mix{layer}",
+    )(part, u, gain, w_out, w_gate, w_up, w_down)
 
 
 def solution(mesh):
@@ -170,19 +338,9 @@
         u = tok_emb.transpose(1, 0, 2).reshape(n_rows, d_model)
         prev = None
         for layer in range(n_layers):
-            o, st, ko, vo = attention(layer, n_steps, offs, u, gain_attn[layer][None], cos_t, sin_t, w_query, w_key, w_value, kc, vc, prev)
+            part, ko, vo = attention(layer, n_steps, offs, u, gain_attn[layer][None], cos_t, sin_t, w_query, w_key, w_value, kc, vc, prev)
             prev = (ko, vo)
-            loc_max = st[:, :n_heads].T[..., None]
-            loc_sum = st[:, 8:8 + n_heads].T[..., None]
-            glob_max = lax.pmax(loc_max, 'sp')
-            merged = lax.psum(jnp.concatenate([o, loc_sum], axis=-1) * jnp.exp(loc_max - glob_max), 'sp')
-            attn_out = (merged[..., :head_dim] / merged[..., head_dim:]).astype(BF16).transpose(1, 0, 2).reshape(n_rows, n_heads * head_dim)
-            proj = lax.psum(jnp.dot(attn_out, w_out[layer], preferred_element_type=F32), 'tp')
-            u = (u.astype(F32) + proj).astype(BF16)
-            h2 = rms_norm(u.astype(F32), gain_mlp[layer].astype(F32))
-            act = (jax.nn.silu(jnp.dot(h2, w_gate[layer], preferred_element_type=F32)) * jnp.dot(h2, w_up[layer], preferred_element_type=F32)).astype(BF16)
-            down = lax.psum(jnp.dot(act, w_down[layer], preferred_element_type=F32), 'tp')
-            u = (u.astype(F32) + down).astype(BF16)
+            u = mix(layer, part, u, gain_mlp[layer][None], w_out, w_gate, w_up, w_down)
         hidden = u.reshape(n_batch, n_steps, d_model).transpose(1, 0, 2)
         return hidden, prev[0].reshape(key_cache.shape), prev[1].reshape(val_cache.shape)
 

time: 316 us -> 102 us (0.32)
  waiting for transfers between devices: 173 us -> 0 us
  Pallas kernels: 26.9 us -> 90.1 us
  matrix products: 48.5 us -> 0 us
  blocking collectives: 25.1 us -> 0 us
  between operations: 14.3 us -> 0.83 us
  other arithmetic: 11.6 us -> 1.84 us
  local copies, waits for them, and re-layouts: 15.4 us -> 8.65 us
    psum x6 -> x0, waiting for transfers between devices: 173 us -> none  [the longest x2 58.6 us: local_fn(): lax.psum(jnp.concatenate([o, loc_sum], axis=-1) * jnp.exp(loc_max - glob_...]
    pallas_call x0 -> x2, Pallas kernels: none -> 62.7 us  [mix(): pl.pallas_call(functools.partial(mix_kernel, layer, n_heads), out_shape=j...]
    dot_general x6 -> x0, matrix products: 48.5 us -> none  [the longest x2 25.5 us: local_fn(): jnp.dot(act, w_down[layer], preferred_element_type=F32)]
    pmax x2 -> x0, blocking collectives: 25.1 us -> none  [local_fn(): glob_max = lax.pmax(loc_max, 'sp')]
    unnamed x14 -> x18, local copies, waits for them, and re-layouts: 6.94 us -> 4.68 us
  transfers between devices with their start and end apart: 6 -> 0, of which waited for: 6 -> 0; matrix products, arithmetic and copies ran while one was open for 0% -> 0% of each run, Pallas kernels for 0% -> 0%
where the time goes in v2:
time: 102 us; the launch traced here: 101 us
  Pallas kernels  90.1 us (88%)
  local copies, waits for them, and re-layouts  8.65 us (8%)
  other arithmetic  1.84 us (2%)
    pallas_call x2, Pallas kernels, mix(): pl.pallas_call(functools.partial(mix_kernel, layer, n_heads), out_shape=j...  62.7 us
    pallas_call x2, Pallas kernels, attention(): pl.pallas_call(functools.partial(attn_kernel, layer, n_steps, n_heads), o...  27.4 us
    unnamed x18, local copies, waits for them, and re-layouts  4.68 us

profile of v2, /device:TPU:0, one launch (start us, length us, event | category | flops | bytes accessed | tf_op | source)
XLA Modules:
  0.0 101.4 jit_solution(9025066399499485691)
XLA Ops:
  0.6 0.7 fusion.2
  1.4 0.8 fusion.4
  2.1 0.8 fusion.3
  2.9 0.7 add_convert_fusion
  3.7 0.1 convert_element_type.18
  3.8 0.3 fusion
  4.1 0.1 pad_maximum_fusion
  4.2 1.3 %copy.22 = bf16[32,4,1536]{2,1,0:T(4,128)(2,1)S(1)} copy(bf16[32,4,1536]{2,0,1:T(8,128)(2,1)} %bitcast.28) | data formatting | bytes 786432 | tf_op jit(solution)/shard_map/transpose | solution.py:338
  5.5 0.0 slice-start
  5.5 0.1 reshape.47.u_ref
  5.6 0.0 copy-start
  5.6 2.4 %copy-done = bf16[2,1536,768]{2,1,0:T(8,128)(2,1)S(1)} copy-done((bf16[2,1536,768]{2,1,0:T(8,128)(2,1)S(1)}, bf16[2,1536,768]{2,1,0:T(8,128)(2,1)}, u32[]{:S(2)}) %copy-start) | copy-done | bytes 4718616
  8.0 0.0 copy-start.1
  8.0 1.1 %copy-done.1 = bf16[2,1536,128]{2,1,0:T(8,128)(2,1)S(1)} copy-done((bf16[2,1536,128]{2,1,0:T(8,128)(2,1)S(1)}, bf16[2,1536,128]{2,1,0:T(8,128)(2,1)}, u32[]{:S(2)}) %copy-start.1) | copy-done | bytes 786456
  9.1 0.0 copy-start.3
  9.1 1.1 %copy-done.3 = bf16[2,1536,128]{2,1,0:T(8,128)(2,1)S(1)} copy-done((bf16[2,1536,128]{2,1,0:T(8,128)(2,1)S(1)}, bf16[2,1536,128]{2,1,0:T(8,128)(2,1)}, u32[]{:S(2)}) %copy-start.3) | copy-done | bytes 786456
  10.3 0.0 slice-start.1
  10.3 0.0 slice-start.2
  10.3 13.9 %attn0.1 = (f32[7,128,128]{2,1,0:T(8,128)S(1)}, bf16[2,32,1024,128]{3,2,1,0:T(8,128)(2,1)}, bf16[2,32,1024,128]{3,2,1,0:T(8,128)(2,1)}) custom-call(s32[3,32]{1,0:T(4,128)S(1)} %pad_add_fusion.offs_ref, bf16[128,1536]{1,0:T(8,128)(2,1)S(1)} %reshape.47.u_ref, bf16[1,1536]{1,0:T(2,128)(2,1)S(1)} %get-tuple-element.26.gain_ref, ...), custom_call_target="tpu_custom_call" | custom-call | tf_op jit(solution)/shard_map/attn0/pallas_call | solution.py:134
  24.2 0.0 slice-done
  24.2 0.0 slice-done.1
  24.2 0.0 slice-start.3
  24.2 0.0 copy-start.2
  24.2 0.0 copy-start.4
  24.2 32.2 %mix0.1.u_ref = bf16[128,1536]{1,0:T(8,128)(2,1)S(1)} custom-call(f32[7,128,128]{2,1,0:T(8,128)S(1)} %get-tuple-element.9.part_ref, bf16[128,1536]{1,0:T(8,128)(2,1)S(1)} %reshape.47.u_ref, bf16[1,1536]{1,0:T(2,128)(2,1)S(1)} %get-tuple-element.24.gain_ref, bf16[2,768,1536]{2,1,0:T(8,128)(2,1)S(1)} %bitcast.19, bf16[2,1536,4480]{2,1,0:T(8,128)(2,1)} %wg_hbm.3, ...), custom_call_target="tpu_custom_call" | custom-call | tf_op jit(solution)/shard_map/mix0/pallas_call | solution.py:300
  56.4 0.0 slice-done.2
  56.4 0.0 slice-done.3
  56.4 0.0 copy-done.2
  56.4 0.0 copy-done.4
  56.5 13.5 %attn1.1 = (f32[7,128,128]{2,1,0:T(8,128)S(1)}, bf16[2,32,1024,128]{3,2,1,0:T(8,128)(2,1)}, bf16[2,32,1024,128]{3,2,1,0:T(8,128)(2,1)}) custom-call(s32[3,32]{1,0:T(4,128)S(1)} %pad_add_fusion.offs_ref, bf16[128,1536]{1,0:T(8,128)(2,1)S(1)} %mix0.1.u_ref, ...), custom_call_target="tpu_custom_call", output_to_operand_aliasing={{1}: (10, {}), {2}: (11, {})} | custom-call | tf_op jit(solution)/shard_map/attn1/pallas_call | solution.py:134
  69.9 30.5 %mix1.1 = bf16[128,1536]{1,0:T(8,128)(2,1)S(1)} custom-call(f32[7,128,128]{2,1,0:T(8,128)S(1)} %get-tuple-element.12.part_ref, bf16[128,1536]{1,0:T(8,128)(2,1)S(1)} %mix0.1.u_ref, bf16[1,1536]{1,0:T(2,128)(2,1)S(1)} %get-tuple-element.23.gain_ref, bf16[2,768,1536]{2,1,0:T(8,128)(2,1)S(1)} %bitcast.19, bf16[2,1536,4480]{2,1,0:T(8,128)(2,1)} %wg_hbm.3, ...), custom_call_target="tpu_custom_call" | custom-call | tf_op jit(solution)/shard_map/mix1/pallas_call | solution.py:300
  100.5 0.1 reshape.50
  100.6 0.8 copy.27
  (5 shorter events, 0.0 us)
Async XLA Ops:
  5.5 18.7 %slice-start = ((s8[4718592]{0:T(1024)(128)(4,1)}), s8[524288]{0:T(1024)(128)(4,1)S(1)}, s32[]{:S(2)}) async-start(s8[4718592]{0:T(1024)(128)(4,1)} %bitcast.18), calls=%async_computation | async-start | bytes 1048576
  5.6 2.4 %copy-start = (bf16[2,1536,768]{2,1,0:T(8,128)(2,1)S(1)}, bf16[2,1536,768]{2,1,0:T(8,128)(2,1)}, u32[]{:S(2)}) copy-start(bf16[2,1536,768]{2,1,0:T(8,128)(2,1)} %wq_hbm.3) | copy-start | bytes 14155780
  8.0 1.1 %copy-start.1 = (bf16[2,1536,128]{2,1,0:T(8,128)(2,1)S(1)}, bf16[2,1536,128]{2,1,0:T(8,128)(2,1)}, u32[]{:S(2)}) copy-start(bf16[2,1536,128]{2,1,0:T(8,128)(2,1)} %wk_hbm.3) | copy-start | bytes 2359300
  9.1 1.1 %copy-start.3 = (bf16[2,1536,128]{2,1,0:T(8,128)(2,1)S(1)}, bf16[2,1536,128]{2,1,0:T(8,128)(2,1)}, u32[]{:S(2)}) copy-start(bf16[2,1536,128]{2,1,0:T(8,128)(2,1)} %wv_hbm.3) | copy-start | bytes 2359300
  10.3 13.9 %slice-start.1 = ((s8[4718592]{0:T(1024)(128)(4,1)}), s8[4194304]{0:T(1024)(128)(4,1)S(1)}, s32[]{:S(2)}) async-start(s8[4718592]{0:T(1024)(128)(4,1)} %bitcast.18), calls=%async_computation.1 | async-start | bytes 8388608
  10.3 46.2 %slice-start.2 = ((s8[4718592]{0:T(1024)(128)(4,1)}), s8[4194304]{0:T(1024)(128)(4,1)S(1)}, s32[]{:S(2)}) async-start(s8[4718592]{0:T(1024)(128)(4,1)} %bitcast.20), calls=%async_computation.2 | async-start | bytes 8388608
  24.2 32.2 %slice-start.3 = ((s8[4718592]{0:T(1024)(128)(4,1)}), s8[524288]{0:T(1024)(128)(4,1)S(1)}, s32[]{:S(2)}) async-start(s8[4718592]{0:T(1024)(128)(4,1)} %bitcast.20), calls=%async_computation.3 | async-start | bytes 1048576
  24.2 32.2 %copy-start.2 = (bf16[2,1536,128]{2,1,0:T(8,128)(2,1)S(1)}, bf16[2,1536,128]{2,1,0:T(8,128)(2,1)}, u32[]{:S(2)}) copy-start(bf16[2,1536,128]{2,1,0:T(8,128)(2,1)} %wk_hbm.3) | copy-start | bytes 2359300
  24.2 32.2 %copy-start.4 = (bf16[2,1536,128]{2,1,0:T(8,128)(2,1)S(1)}, bf16[2,1536,128]{2,1,0:T(8,128)(2,1)}, u32[]{:S(2)}) copy-start(bf16[2,1536,128]{2,1,0:T(8,128)(2,1)} %wv_hbm.3) | copy-start | bytes 2359300

commit v3 on v2

--- a/solution.py
+++ b/solution.py
@@ -1,6 +1,7 @@
 import functools
 import jax
 import jax.numpy as jnp
+import numpy as np
 from jax import lax
 from jax.experimental import pallas as pl
 from jax.experimental.pallas import tpu as pltpu
@@ -11,6 +12,8 @@
 F32 = jnp.float32
 BF16 = jnp.bfloat16
 MESH = pl.DeviceIdType.MESH
+ATTN_VMEM = 40 * 1024 * 1024
+MIX_VMEM = 48 * 1024 * 1024
 
 
 def rms_norm(x_float, gain_row):
@@ -18,18 +21,25 @@
     return (x_float * inv_rms * gain_row).astype(BF16)
 
 
-def attn_kernel(layer, n_steps, n_heads, offs_ref, u_ref, gain_ref, cos_ref, sin_ref, wq_hbm, wk_hbm, wv_hbm, kc_hbm, vc_hbm, *rest):
+def attn_kernel(layer, n_steps, n_heads, len_hbm, u_in, gain_hbm, freq_hbm, wq_hbm, wk_hbm, wv_hbm, kc_hbm, vc_hbm, *rest):
     if layer > 0:
         rest = rest[2:]
-    o_ref, ko_hbm, vo_hbm, wq_buf, wk_buf, wv_buf, kbuf, vbuf, q_sc, kn_sc, vn_sc, w_sem, in_sem, out_sem = rest
-    n_rows = u_ref.shape[0]
+        o_ref, ko_hbm, vo_hbm = rest[:3]
+    else:
+        o_ref, ko_hbm, vo_hbm, u_perm = rest[:4]
+        rest = rest[1:]
+    wq_buf, wk_buf, wv_buf, kbuf, vbuf, q_sc, kn_sc, vn_sc, len_ref, gain_ref, freq_ref, u_buf, w_sem, in_sem, out_sem = rest[3:]
+    sp = lax.axis_index('sp')
+    n_rows = u_in.shape[0]
     n_slots, head_dim = kbuf.shape[1], kbuf.shape[2]
     n_seq = kbuf.shape[0]
     n_pairs = n_seq // 2
     pair_rows = 2 * n_steps
 
     w_copies = [pltpu.make_async_copy(src.at[layer], dst, w_sem.at[i]) for i, (src, dst) in enumerate(((wq_hbm, wq_buf), (wk_hbm, wk_buf), (wv_hbm, wv_buf)))]
-    for cp in w_copies:
+    smalls = [(len_hbm, len_ref), (gain_hbm, gain_ref), (freq_hbm, freq_ref)] + ([(u_in, u_buf)] if layer == 0 else [])
+    smalls = [pltpu.make_async_copy(src, dst, w_sem.at[3 + i]) for i, (src, dst) in enumerate(smalls)]
+    for cp in smalls + w_copies:
         cp.start()
 
     def in_copies(i):
@@ -47,9 +57,24 @@
         for cp in in_copies(i):
             cp.start()
 
-    h = rms_norm(u_ref[...].astype(F32), gain_ref[...].astype(F32))
-    cos_t = cos_ref[...]
-    sin_t = sin_ref[...]
+    for cp in smalls:
+        cp.wait()
+    if layer == 0:
+        row = lax.broadcasted_iota(jnp.int32, (n_rows, n_rows), 0)
+        col = lax.broadcasted_iota(jnp.int32, (n_rows, n_rows), 1)
+        perm = jnp.where(col == (row % n_steps) * n_seq + row // n_steps, 1.0, 0.0).astype(BF16)
+        u = jnp.dot(perm, u_buf[...], preferred_element_type=F32)
+        u_perm[...] = u.astype(BF16)
+    else:
+        u = u_in[...].astype(F32)
+    h = rms_norm(u, gain_ref[layer:layer + 1, :].astype(F32))
+    sub8 = lax.broadcasted_iota(jnp.int32, (pair_rows, head_dim), 0)
+    pos = jnp.concatenate([jnp.where(sub8 < n_steps, len_ref[2 * i], len_ref[2 * i + 1]) + sub8 % n_steps for i in range(n_pairs)], axis=0)
+    angles = pos.astype(F32) * freq_ref[...]
+    lane = lax.broadcasted_iota(jnp.int32, angles.shape, 1)
+    cos_t = jnp.cos(angles)
+    sin_t = jnp.sin(angles)
+    sin_t = jnp.where(lane < head_dim // 2, -sin_t, sin_t)
 
     def rope(x):
         return (x * cos_t + pltpu.roll(x, head_dim // 2, 1) * sin_t).astype(BF16).astype(F32)
@@ -74,9 +99,10 @@
         scs = []
         for e in range(2):
             b = 2 * i + e
-            off = offs_ref[0, b]
-            slot = offs_ref[1, b]
-            row = offs_ref[2, b]
+            step = (len_ref[b] + (4 - sp)) & 3
+            step = (4 - step) & 3
+            slot = (len_ref[b] + step) // 4
+            row = n_steps * b + step
             base = pl.multiple_of((slot // 16) * 16, 16)
             hit = lax.broadcasted_iota(jnp.int32, (16, head_dim), 0) == slot - base
             for buf, new in ((kbuf, kn_sc), (vbuf, vn_sc)):
@@ -84,7 +110,7 @@
                 new_row = new[pl.ds(row, 1), :]
                 buf[b, pl.ds(base, 16), :] = jnp.where(hit, jnp.broadcast_to(new_row, (16, head_dim)), tile).astype(BF16)
             scs.append(lax.dot_general(q48, kbuf[b], (((1,), (1,)), ((), ())), preferred_element_type=F32))
-        lim = (jnp.where(first, offs_ref[0, 2 * i] + sub, offs_ref[0, 2 * i + 1] + sub - n_steps)) // 4
+        lim = (jnp.where(first, len_ref[2 * i] + sub, len_ref[2 * i + 1] + sub - n_steps) - sp) // 4
         s = jnp.where(jnp.broadcast_to(first, scs[0].shape), scs[0], scs[1]) * scale
         slot_id = lax.broadcasted_iota(jnp.int32, s.shape, 1)
         s = jnp.where(slot_id <= lim, s, -1e30)
@@ -116,34 +142,35 @@
             cp.wait()
 
 
-def attention(layer, n_steps, offs, u, gain, cos_t, sin_t, w_query, w_key, w_value, kc, vc, prev):
+def attention(layer, n_steps, lengths, u, gain, freq, w_query, w_key, w_value, kc, vc, prev):
     n_layers, n_seq, n_slots, head_dim = kc.shape
     n_rows, d_model = u.shape
     q_cols = w_query.shape[2]
     n_heads = q_cols // head_dim
-    any_spec = pl.BlockSpec(memory_space=pl.ANY)
+    any_spec = pl.BlockSpec(memory_space=pltpu.HBM)
     vm = pl.BlockSpec(memory_space=pltpu.VMEM)
-    ins = [offs, u, gain, cos_t, sin_t, w_query, w_key, w_value, kc, vc]
-    in_specs = [pl.BlockSpec(memory_space=pltpu.SMEM), vm, vm, vm, vm] + [any_spec] * 5
+    ins = [lengths, u, gain, freq, w_query, w_key, w_value, kc, vc]
+    in_specs = [any_spec, any_spec if layer == 0 else vm, any_spec, any_spec] + [any_spec] * 5
     aliases = {}
     if layer > 0:
         ins += list(prev)
         in_specs += [any_spec] * 2
-        aliases = {10: 1, 11: 2}
+        aliases = {9: 1, 10: 2}
     cache_t = jax.ShapeDtypeStruct(kc.shape, kc.dtype)
     return pl.pallas_call(
         functools.partial(attn_kernel, layer, n_steps, n_heads),
-        out_shape=[jax.ShapeDtypeStruct((n_heads + 1, n_rows, head_dim), F32), cache_t, cache_t],
+        out_shape=[jax.ShapeDtypeStruct((n_heads + 1, n_rows, head_dim), F32), cache_t, cache_t] + ([jax.ShapeDtypeStruct(u.shape, BF16)] if layer == 0 else []),
         in_specs=in_specs,
-        out_specs=[vm, any_spec, any_spec],
+        out_specs=[vm, any_spec, any_spec] + ([vm] if layer == 0 else []),
         scratch_shapes=[
             pltpu.VMEM((d_model, q_cols), BF16), pltpu.VMEM((d_model, head_dim), BF16), pltpu.VMEM((d_model, head_dim), BF16),
             pltpu.VMEM((n_seq, n_slots, head_dim), BF16), pltpu.VMEM((n_seq, n_slots, head_dim), BF16),
             pltpu.VMEM((n_heads, n_rows, head_dim), F32), pltpu.VMEM((n_rows, head_dim), F32), pltpu.VMEM((n_rows, head_dim), F32),
-            pltpu.SemaphoreType.DMA((3,)), pltpu.SemaphoreType.DMA((2, n_seq // 2)), pltpu.SemaphoreType.DMA((2, n_seq // 2)),
+            pltpu.SMEM(lengths.shape, jnp.int32), pltpu.VMEM(gain.shape, BF16), pltpu.VMEM(freq.shape, F32), pltpu.VMEM(u.shape if layer == 0 else (16, 128), BF16),
+            pltpu.SemaphoreType.DMA((7,)), pltpu.SemaphoreType.DMA((2, n_seq // 2)), pltpu.SemaphoreType.DMA((2, n_seq // 2)),
         ],
         input_output_aliases=aliases,
-        compiler_params=pltpu.CompilerParams(vmem_limit_bytes=40 * 1024 * 1024),
+        compiler_params=pltpu.CompilerParams(vmem_limit_bytes=ATTN_VMEM),
         name=f"attn{layer}",
     )(*ins)
 
@@ -161,9 +188,9 @@
     return outs, st
 
 
-def mix_kernel(layer, n_heads, part_ref, u_ref, gain_ref, wo_hbm, wg_hbm, wu_hbm, wd_hbm, out_ref,
+def mix_kernel(layer, n_heads, part_ref, u_ref, gain_hbm, wo_hbm, wg_hbm, wu_hbm, wd_hbm, out_ref,
                wo_buf, wg_buf, wu_buf, wd_buf, core_in, fwd_out, fwd_in, y_out, y_in, u1_sc, h_out, h_in, hh, act,
-               d_own, d_out, d_in, e_out, e_in, u_all, w_sem, send_sem, recv_sem):
+               d_own, d_out, d_in, e_out, e_in, u_all, gain_ref, w_sem, send_sem, recv_sem):
     tp = lax.axis_index('tp')
     sp = lax.axis_index('sp')
     core = lax.rem(sp, 2)
@@ -180,6 +207,7 @@
         pltpu.make_async_copy(wg_hbm.at[layer, :, pl.ds(col0, ff)], wg_buf, w_sem.at[1]),
         pltpu.make_async_copy(wu_hbm.at[layer, :, pl.ds(col0, ff)], wu_buf, w_sem.at[2]),
         pltpu.make_async_copy(wd_hbm.at[layer, pl.ds(col0, ff), :], wd_buf, w_sem.at[3]),
+        pltpu.make_async_copy(gain_hbm, gain_ref, w_sem.at[4]),
     ]
     for cp in w_copies:
         cp.start()
@@ -225,6 +253,7 @@
 
     y_copies = [remote(y_out.at[n], y_in.at[n], tp_peer) for n in range(n_blk)]
     w_copies[0].wait()
+    w_copies[4].wait()
     for n in range(n_blk):
         y_out[n] = jnp.dot(attn_out, wo_buf[:, n * width:(n + 1) * width], preferred_element_type=F32)
         y_copies[n].start()
@@ -232,12 +261,12 @@
         y_copies[n].wait_recv()
         cols = slice(n * width, (n + 1) * width)
         u1_sc[:, cols] = (u_ref[rows(sp), cols].astype(F32) + (y_out[n] + y_in[n])).astype(BF16).astype(F32)
-    h2 = rms_norm(u1_sc[...], gain_ref[...].astype(F32))
+    h2 = rms_norm(u1_sc[...], gain_ref[layer:layer + 1, :].astype(F32))
     h_out[...] = h2.astype(F32)
     hh[0:chunk, :] = h2
     h_copy = remote(h_out, h_in, core_peer)
     h_copy.start()
-    for cp in w_copies[1:]:
+    for cp in w_copies[1:4]:
         cp.wait()
     h_copy.wait_recv()
     hh[chunk:2 * chunk, :] = h_in[...].astype(BF16)
@@ -290,9 +319,9 @@
     chunk = n_rows // 4
     n_tiles = w_gate.shape[2] // 128
     ff = ((n_tiles + 1) // 2) * 128
-    n_blk = 3
+    n_blk = 6
     width = d_model // n_blk
-    any_spec = pl.BlockSpec(memory_space=pl.ANY)
+    any_spec = pl.BlockSpec(memory_space=pltpu.HBM)
     vm = pl.BlockSpec(memory_space=pltpu.VMEM)
     blocks = pltpu.VMEM((n_blk, chunk, width), F32)
     planes = pltpu.VMEM((n_planes, chunk, head_dim), F32)
@@ -300,7 +329,7 @@
     return pl.pallas_call(
         functools.partial(mix_kernel, layer, n_heads),
         out_shape=jax.ShapeDtypeStruct((n_rows, d_model), BF16),
-        in_specs=[vm, vm, vm] + [any_spec] * 4,
+        in_specs=[vm, vm] + [any_spec] * 5,
         out_specs=vm,
         scratch_shapes=[
             pltpu.VMEM((w_out.shape[1], d_model), BF16), pltpu.VMEM((d_model, ff), BF16), pltpu.VMEM((d_model, ff), BF16), pltpu.VMEM((ff, d_model), BF16),
@@ -308,39 +337,37 @@
             blocks, blocks, pltpu.VMEM((chunk, d_model), F32), pltpu.VMEM((chunk, d_model), F32), pltpu.VMEM((chunk, d_model), F32),
             pltpu.VMEM((2 * chunk, d_model), BF16), pltpu.VMEM((2 * chunk, ff), BF16),
             blocks, blocks, blocks, blocks, blocks, pltpu.VMEM((n_blk, n_rows, width), F32),
-            pltpu.SemaphoreType.DMA((4,)), pltpu.SemaphoreType.DMA((n_copies,)), pltpu.SemaphoreType.DMA((n_copies,)),
+            pltpu.VMEM(gain.shape, BF16), pltpu.SemaphoreType.DMA((5,)), pltpu.SemaphoreType.DMA((n_copies,)), pltpu.SemaphoreType.DMA((n_copies,)),
         ],
-        compiler_params=pltpu.CompilerParams(collective_id=layer, has_side_effects=True, vmem_limit_bytes=48 * 1024 * 1024),
+        compiler_params=pltpu.CompilerParams(collective_id=layer, has_side_effects=True, vmem_limit_bytes=MIX_VMEM),
         name=f"mix{layer}",
     )(part, u, gain, w_out, w_gate, w_up, w_down)
 
 
+def in_hbm(x):
+    return pltpu.with_memory_space_constraint(x, pltpu.HBM)
+
+
 def solution(mesh):
-    sp_size = mesh.shape['sp']
-
     def local_fn(tok_emb, lengths, key_cache, val_cache, gain_attn, gain_mlp, w_query, w_key, w_value, w_out, w_gate, w_up, w_down):
         n_steps, n_batch, d_model = tok_emb.shape
         n_layers, _, loc_len, kv_loc, head_dim = key_cache.shape
-        n_heads = w_query.shape[2] // head_dim
         n_rows = n_steps * n_batch
-        my_sp = lax.axis_index('sp')
         kc = key_cache.reshape(n_layers, n_batch, loc_len, head_dim)
         vc = val_cache.reshape(n_layers, n_batch, loc_len, head_dim)
-        own_step = (my_sp - lengths) % sp_size
-        offs = jnp.stack([lengths - my_sp, (lengths + own_step) // sp_size, jnp.arange(n_batch, dtype=jnp.int32) * n_steps + own_step]).astype(jnp.int32)
-        positions = (lengths[:, None] + jnp.arange(n_steps)[None, :]).reshape(n_rows)
-        half_dim = head_dim // 2
-        inv_freq = 1.0 / (ROPE_BASE ** (jnp.arange(half_dim).astype(F32) * 2.0 / head_dim))
-        angles = positions.astype(F32)[:, None] * inv_freq[None, :]
-        cos_a, sin_a = jnp.cos(angles), jnp.sin(angles)
-        cos_t = jnp.concatenate([cos_a, cos_a], axis=-1)
-        sin_t = jnp.concatenate([-sin_a, sin_a], axis=-1)
-        u = tok_emb.transpose(1, 0, 2).reshape(n_rows, d_model)
+        half = np.arange(head_dim // 2, dtype=np.float32) * np.float32(2.0) / np.float32(head_dim)
+        freq = np.float32(1.0) / np.power(np.float32(ROPE_BASE), half)
+        freq = jnp.asarray(np.concatenate([freq, freq])[None], F32)
+        u = tok_emb.reshape(n_rows, d_model)
+        u, lengths, freq, gain_attn, gain_mlp, kc, vc = map(in_hbm, (u, lengths, freq, gain_attn, gain_mlp, kc, vc))
+        w_query, w_key, w_value, w_out, w_gate, w_up, w_down = map(in_hbm, (w_query, w_key, w_value, w_out, w_gate, w_up, w_down))
         prev = None
         for layer in range(n_layers):
-            part, ko, vo = attention(layer, n_steps, offs, u, gain_attn[layer][None], cos_t, sin_t, w_query, w_key, w_value, kc, vc, prev)
-            prev = (ko, vo)
-            u = mix(layer, part, u, gain_mlp[layer][None], w_out, w_gate, w_up, w_down)
+            res = attention(layer, n_steps, lengths, u, gain_attn, freq, w_query, w_key, w_value, kc, vc, prev)
+            part, prev = res[0], res[1:3]
+            if layer == 0:
+                u = res[3]
+            u = mix(layer, part, u, gain_mlp, w_out, w_gate, w_up, w_down)
         hidden = u.reshape(n_batch, n_steps, d_model).transpose(1, 0, 2)
         return hidden, prev[0].reshape(key_cache.shape), prev[1].reshape(val_cache.shape)
 

time: 102 us -> 92.8 us (0.910)
  local copies, waits for them, and re-layouts: 8.65 us -> 0.91 us
  other arithmetic: 1.84 us -> 0 us
    unnamed x18 -> x0, local copies, waits for them, and re-layouts: 4.68 us -> none
    pallas_call x2, Pallas kernels: 62.7 us -> 64.3 us  [mix(): pl.pallas_call(functools.partial(mix_kernel, layer, n_heads), out_shape=j...]
    slice x2 -> x0, local copies, waits for them, and re-layouts: 1.57 us -> none  [the longest x1 0.78 us: local_fn(): gain_attn[layer][None]]
    transpose x1 -> x0, local copies, waits for them, and re-layouts: 1.3 us -> none  [local_fn(): u = tok_emb.transpose(1, 0, 2).reshape(n_rows, d_model)]
where the time goes in v3:
time: 92.8 us; the launch traced here: 92.7 us
  Pallas kernels  91.1 us (98%)
    pallas_call x2, Pallas kernels, mix(): pl.pallas_call(functools.partial(mix_kernel, layer, n_heads), out_shape=j...  64.3 us
    pallas_call x2, Pallas kernels, attention(): pl.pallas_call(functools.partial(attn_kernel, layer, n_steps, n_heads), o...  26.8 us

profile of v3, /device:TPU:0, one launch (start us, length us, event | category | flops | bytes accessed | tf_op | source)
XLA Modules:
  0.0 92.7 jit_solution(14716511862839394349)
XLA Ops:
  0.6 13.4 %attn0.1 = (f32[7,128,128]{2,1,0:T(8,128)S(1)}, bf16[2,32,1024,128]{3,2,1,0:T(8,128)(2,1)}, bf16[2,32,1024,128]{3,2,1,0:T(8,128)(2,1)}, bf16[128,1536]{1,0:T(8,128)(2,1)S(1)}) custom-call(s32[32]{0:T(128)} %len_hbm.3, bf16[128,1536]{1,0:T(8,128)(2,1)} %bitcast.18, bf16[2,1536]{1,0:T(2,128)(2,1)} %gain_hbm.6, f32[1,128]{1,0:T(1,128)} %constant.2.clone.freq_hbm, ...), custom_call_target="tpu_custom_call" | custom-call | tf_op jit(solution)/shard_map/attn0/pallas_call | solution.py:160
  14.1 32.3 %mix0.1.u_in.u_ref = bf16[128,1536]{1,0:T(8,128)(2,1)S(1)} custom-call(f32[7,128,128]{2,1,0:T(8,128)S(1)} %get-tuple-element.10.part_ref, bf16[128,1536]{1,0:T(8,128)(2,1)S(1)} %get-tuple-element.11.u_ref, bf16[2,1536]{1,0:T(2,128)(2,1)} %gain_hbm.7, bf16[2,768,1536]{2,1,0:T(8,128)(2,1)} %wo_hbm.3, bf16[2,1536,4480]{2,1,0:T(8,128)(2,1)} %wg_hbm.3, ...), custom_call_target="tpu_custom_call" | custom-call | tf_op jit(solution)/shard_map/mix0/pallas_call | solution.py:329
  46.4 13.3 %attn1.1 = (f32[7,128,128]{2,1,0:T(8,128)S(1)}, bf16[2,32,1024,128]{3,2,1,0:T(8,128)(2,1)}, bf16[2,32,1024,128]{3,2,1,0:T(8,128)(2,1)}) custom-call(s32[32]{0:T(128)} %len_hbm.3, bf16[128,1536]{1,0:T(8,128)(2,1)S(1)} %mix0.1.u_in.u_ref, bf16[2,1536]{1,0:T(2,128)(2,1)} %gain_hbm.6, ...), custom_call_target="tpu_custom_call", output_to_operand_aliasing={{1}: (9, {}), {2}: (10, {})} | custom-call | tf_op jit(solution)/shard_map/attn1/pallas_call | solution.py:160
  59.7 32.0 %mix1.1 = bf16[128,1536]{1,0:T(8,128)(2,1)S(1)} custom-call(f32[7,128,128]{2,1,0:T(8,128)S(1)} %get-tuple-element.14.part_ref, bf16[128,1536]{1,0:T(8,128)(2,1)S(1)} %mix0.1.u_in.u_ref, bf16[2,1536]{1,0:T(2,128)(2,1)} %gain_hbm.7, bf16[2,768,1536]{2,1,0:T(8,128)(2,1)} %wo_hbm.3, bf16[2,1536,4480]{2,1,0:T(8,128)(2,1)} %wg_hbm.3, ...), custom_call_target="tpu_custom_call" | custom-call | tf_op jit(solution)/shard_map/mix1/pallas_call | solution.py:329
  91.8 0.1 reshape.27
  91.9 0.8 copy.23

commit v4 on v3

--- a/solution.py
+++ b/solution.py
@@ -12,8 +12,6 @@
 F32 = jnp.float32
 BF16 = jnp.bfloat16
 MESH = pl.DeviceIdType.MESH
-ATTN_VMEM = 40 * 1024 * 1024
-MIX_VMEM = 48 * 1024 * 1024
 
 
 def rms_norm(x_float, gain_row):
@@ -21,60 +19,66 @@
     return (x_float * inv_rms * gain_row).astype(BF16)
 
 
-def attn_kernel(layer, n_steps, n_heads, len_hbm, u_in, gain_hbm, freq_hbm, wq_hbm, wk_hbm, wv_hbm, kc_hbm, vc_hbm, *rest):
-    if layer > 0:
-        rest = rest[2:]
-        o_ref, ko_hbm, vo_hbm = rest[:3]
-    else:
-        o_ref, ko_hbm, vo_hbm, u_perm = rest[:4]
-        rest = rest[1:]
-    wq_buf, wk_buf, wv_buf, kbuf, vbuf, q_sc, kn_sc, vn_sc, len_ref, gain_ref, freq_ref, u_buf, w_sem, in_sem, out_sem = rest[3:]
+def attn_kernel(layer, n_steps, n_heads, names, *refs):
+    r = dict(zip(names, refs))
+    len_ref, gain_ref, freq_ref, q_sc, kn_sc, vn_sc, o_ref = (r[k] for k in ('len', 'gain', 'freq', 'q_sc', 'kn_sc', 'vn_sc', 'part'))
+    kbuf, vbuf, wq_buf, wk_buf, wv_buf, w_sem, in_sem, out_sem = (r[k] for k in ('kbuf', 'vbuf', 'wq_buf', 'wk_buf', 'wv_buf', 'w_sem', 'in_sem', 'out_sem'))
+    ko_hbm, vo_hbm = r['ko'], r['vo']
+    u_in = r['u_in']
     sp = lax.axis_index('sp')
     n_rows = u_in.shape[0]
     n_slots, head_dim = kbuf.shape[1], kbuf.shape[2]
     n_seq = kbuf.shape[0]
     n_pairs = n_seq // 2
     pair_rows = 2 * n_steps
-
-    w_copies = [pltpu.make_async_copy(src.at[layer], dst, w_sem.at[i]) for i, (src, dst) in enumerate(((wq_hbm, wq_buf), (wk_hbm, wk_buf), (wv_hbm, wv_buf)))]
-    smalls = [(len_hbm, len_ref), (gain_hbm, gain_ref), (freq_hbm, freq_ref)] + ([(u_in, u_buf)] if layer == 0 else [])
-    smalls = [pltpu.make_async_copy(src, dst, w_sem.at[3 + i]) for i, (src, dst) in enumerate(smalls)]
-    for cp in smalls + w_copies:
+    first_layer = layer == 0
+
+    copies = [(r['len_in'], len_ref), (r['gain_in'], gain_ref)]
+    if first_layer:
+        copies += [(r['freq_in'], freq_ref), (u_in, r['u_buf']), (r['wq_in'].at[layer], wq_buf), (r['wk_in'].at[layer], wk_buf), (r['wv_in'].at[layer], wv_buf)]
+    copies = [pltpu.make_async_copy(src, dst, w_sem.at[i]) for i, (src, dst) in enumerate(copies)]
+    smalls, w_copies = copies[:4], copies[4:]
+    for cp in copies:
         cp.start()
 
     def in_copies(i):
         sl = pl.ds(2 * i, 2)
-        return (pltpu.make_async_copy(kc_hbm.at[layer, sl], kbuf.at[sl], in_sem.at[0, i]),
-                pltpu.make_async_copy(vc_hbm.at[layer, sl], vbuf.at[sl], in_sem.at[1, i]))
+        return (pltpu.make_async_copy(r['kc'].at[layer, sl], kbuf.at[sl], in_sem.at[0, i]),
+                pltpu.make_async_copy(r['vc'].at[layer, sl], vbuf.at[sl], in_sem.at[1, i]))
 
     def out_copies(i):
         sl = pl.ds(2 * i, 2)
-        return (pltpu.make_async_copy(kbuf.at[sl], ko_hbm.at[layer, sl], out_sem.at[0, i]),
-                pltpu.make_async_copy(vbuf.at[sl], vo_hbm.at[layer, sl], out_sem.at[1, i]))
-
-    @pl.loop(0, n_pairs)
-    def _(i):
-        for cp in in_copies(i):
-            cp.start()
+        return (pltpu.make_async_copy(kbuf.at[sl], ko_hbm.at[layer, sl], out_sem.at[0]),
+                pltpu.make_async_copy(vbuf.at[sl], vo_hbm.at[layer, sl], out_sem.at[1]))
+
+    if first_layer:
+        @pl.loop(0, n_pairs)
+        def _(i):
+            for cp in in_copies(i):
+                cp.start()
 
     for cp in smalls:
         cp.wait()
-    if layer == 0:
+    if first_layer:
         row = lax.broadcasted_iota(jnp.int32, (n_rows, n_rows), 0)
         col = lax.broadcasted_iota(jnp.int32, (n_rows, n_rows), 1)
         perm = jnp.where(col == (row % n_steps) * n_seq + row // n_steps, 1.0, 0.0).astype(BF16)
-        u = jnp.dot(perm, u_buf[...], preferred_element_type=F32)
-        u_perm[...] = u.astype(BF16)
+        u = jnp.dot(perm, r['u_buf'][...], preferred_element_type=F32)
+        r['u_perm'][...] = u.astype(BF16)
     else:
         u = u_in[...].astype(F32)
     h = rms_norm(u, gain_ref[layer:layer + 1, :].astype(F32))
-    sub8 = lax.broadcasted_iota(jnp.int32, (pair_rows, head_dim), 0)
-    pos = jnp.concatenate([jnp.where(sub8 < n_steps, len_ref[2 * i], len_ref[2 * i + 1]) + sub8 % n_steps for i in range(n_pairs)], axis=0)
-    angles = pos.astype(F32) * freq_ref[...]
-    lane = lax.broadcasted_iota(jnp.int32, angles.shape, 1)
-    cos_t = jnp.cos(angles)
-    sin_t = jnp.sin(angles)
-    sin_t = jnp.where(lane < head_dim // 2, -sin_t, sin_t)
+    cos_ref, sin_ref = r['cos'], r['sin']
+    if first_layer:
+        sub8 = lax.broadcasted_iota(jnp.int32, (pair_rows, head_dim), 0)
+        pos = jnp.concatenate([jnp.where(sub8 < n_steps, len_ref[2 * i], len_ref[2 * i + 1]) + sub8 % n_steps for i in range(n_pairs)], axis=0)
+        angles = pos.astype(F32) * freq_ref[...]
+        lane = lax.broadcasted_iota(jnp.int32, angles.shape, 1)
+        cos_ref[...] = jnp.cos(angles)
+        sin_t = jnp.sin(angles)
+        sin_ref[...] = jnp.where(lane < head_dim // 2, -sin_t, sin_t)
+    cos_t = cos_ref[...]
+    sin_t = sin_ref[...]
 
     def rope(x):
         return (x * cos_t + pltpu.roll(x, head_dim // 2, 1) * sin_t).astype(BF16).astype(F32)
@@ -91,8 +95,9 @@
     scale = head_dim ** -0.5
 
     def pair_body(i):
-        for cp in in_copies(i):
-            cp.wait()
+        if first_layer:
+            for cp in in_copies(i):
+                cp.wait()
         sub = lax.broadcasted_iota(jnp.int32, (m_rows, 1), 0) % pair_rows
         first = sub < n_steps
         q48 = jnp.concatenate([q_sc[hd, pl.ds(pair_rows * i, pair_rows), :] for hd in range(n_heads)], axis=0).astype(BF16)
@@ -142,37 +147,50 @@
             cp.wait()
 
 
-def attention(layer, n_steps, lengths, u, gain, freq, w_query, w_key, w_value, kc, vc, prev):
-    n_layers, n_seq, n_slots, head_dim = kc.shape
+def attention(layer, n_steps, n_heads, lengths, u, gain, ins):
     n_rows, d_model = u.shape
-    q_cols = w_query.shape[2]
-    n_heads = q_cols // head_dim
-    any_spec = pl.BlockSpec(memory_space=pltpu.HBM)
+    head_dim = 128
+    hbm = pl.BlockSpec(memory_space=pltpu.HBM)
     vm = pl.BlockSpec(memory_space=pltpu.VMEM)
-    ins = [lengths, u, gain, freq, w_query, w_key, w_value, kc, vc]
-    in_specs = [any_spec, any_spec if layer == 0 else vm, any_spec, any_spec] + [any_spec] * 5
-    aliases = {}
-    if layer > 0:
-        ins += list(prev)
-        in_specs += [any_spec] * 2
-        aliases = {9: 1, 10: 2}
-    cache_t = jax.ShapeDtypeStruct(kc.shape, kc.dtype)
-    return pl.pallas_call(
-        functools.partial(attn_kernel, layer, n_steps, n_heads),
-        out_shape=[jax.ShapeDtypeStruct((n_heads + 1, n_rows, head_dim), F32), cache_t, cache_t] + ([jax.ShapeDtypeStruct(u.shape, BF16)] if layer == 0 else []),
-        in_specs=in_specs,
-        out_specs=[vm, any_spec, any_spec] + ([vm] if layer == 0 else []),
-        scratch_shapes=[
-            pltpu.VMEM((d_model, q_cols), BF16), pltpu.VMEM((d_model, head_dim), BF16), pltpu.VMEM((d_model, head_dim), BF16),
-            pltpu.VMEM((n_seq, n_slots, head_dim), BF16), pltpu.VMEM((n_seq, n_slots, head_dim), BF16),
-            pltpu.VMEM((n_heads, n_rows, head_dim), F32), pltpu.VMEM((n_rows, head_dim), F32), pltpu.VMEM((n_rows, head_dim), F32),
-            pltpu.SMEM(lengths.shape, jnp.int32), pltpu.VMEM(gain.shape, BF16), pltpu.VMEM(freq.shape, F32), pltpu.VMEM(u.shape if layer == 0 else (16, 128), BF16),
-            pltpu.SemaphoreType.DMA((7,)), pltpu.SemaphoreType.DMA((2, n_seq // 2)), pltpu.SemaphoreType.DMA((2, n_seq // 2)),
-        ],
+    first_layer = layer == 0
+    n_seq = n_rows // n_steps
+    tile = jax.ShapeDtypeStruct((n_rows, head_dim), F32)
+    part = jax.ShapeDtypeStruct((n_heads + 1, n_rows, head_dim), F32)
+    scratch = {'len': pltpu.SMEM(lengths.shape, jnp.int32), 'gain': pltpu.VMEM(gain.shape, BF16), 'q_sc': pltpu.VMEM((n_heads, n_rows, head_dim), F32),
+               'kn_sc': pltpu.VMEM((n_rows, head_dim), F32), 'vn_sc': pltpu.VMEM((n_rows, head_dim), F32), 'w_sem': pltpu.SemaphoreType.DMA((7,)), 'out_sem': pltpu.SemaphoreType.DMA((2,))}
+    if first_layer:
+        freq, w_query, w_key, w_value, kc, vc = ins
+        cache_t = jax.ShapeDtypeStruct(kc.shape, kc.dtype)
+        args = {'len_in': lengths, 'u_in': u, 'gain_in': gain, 'freq_in': freq, 'wq_in': w_query, 'wk_in': w_key, 'wv_in': w_value, 'kc': kc, 'vc': vc}
+        specs = {k: hbm for k in args}
+        outs = {'part': (part, vm), 'ko': (cache_t, hbm), 'vo': (cache_t, hbm), 'u_perm': (jax.ShapeDtypeStruct(u.shape, BF16), vm), 'cos': (tile, vm), 'sin': (tile, vm)}
+        scratch.update({'freq': pltpu.VMEM(freq.shape, F32), 'u_buf': pltpu.VMEM(u.shape, BF16), 'kbuf': pltpu.VMEM(kc.shape[1:], BF16), 'vbuf': pltpu.VMEM(kc.shape[1:], BF16),
+                        'wq_buf': pltpu.VMEM(w_query.shape[1:], BF16), 'wk_buf': pltpu.VMEM(w_key.shape[1:], BF16), 'wv_buf': pltpu.VMEM(w_value.shape[1:], BF16),
+                        'in_sem': pltpu.SemaphoreType.DMA((2, n_seq // 2))})
+        aliases = {}
+    else:
+        cos_t, sin_t, ko, vo, k_loc, v_loc, wq, wk, wv = ins
+        cache_t = jax.ShapeDtypeStruct(ko.shape, ko.dtype)
+        loc_t = pltpu.VMEM(k_loc.shape, BF16)
+        k_loc, v_loc, wq, wk, wv = map(in_vmem, (k_loc, v_loc, wq, wk, wv))
+        args = {'len_in': lengths, 'u_in': u, 'gain_in': gain, 'cos': cos_t, 'sin': sin_t, 'wq_buf': wq, 'wk_buf': wk, 'wv_buf': wv, 'ko_in': ko, 'vo_in': vo, 'k_loc': k_loc, 'v_loc': v_loc}
+        specs = {k: hbm if k in ('len_in', 'gain_in', 'ko_in', 'vo_in') else vm for k in args}
+        outs = {'part': (part, vm), 'ko': (cache_t, hbm), 'vo': (cache_t, hbm), 'kbuf': (loc_t, vm), 'vbuf': (loc_t, vm)}
+        scratch.update({'freq': pltpu.SMEM((1,), jnp.int32), 'in_sem': pltpu.SemaphoreType.DMA((1,))})
+        order = list(args)
+        aliases = {order.index('ko_in'): 1, order.index('vo_in'): 2, order.index('k_loc'): 3, order.index('v_loc'): 4}
+    names = list(args) + list(outs) + list(scratch)
+    res = pl.pallas_call(
+        functools.partial(attn_kernel, layer, n_steps, n_heads, names),
+        out_shape=[o[0] for o in outs.values()],
+        in_specs=list(specs.values()),
+        out_specs=[o[1] for o in outs.values()],
+        scratch_shapes=list(scratch.values()),
         input_output_aliases=aliases,
-        compiler_params=pltpu.CompilerParams(vmem_limit_bytes=ATTN_VMEM),
+        compiler_params=pltpu.CompilerParams(vmem_limit_bytes=(32 if first_layer else 8) * 1024 * 1024),
         name=f"attn{layer}",
-    )(*ins)
+    )(*args.values())
+    return dict(zip(outs, res))
 
 
 def merge(a, b, n_heads):
@@ -188,7 +206,12 @@
     return outs, st
 
 
-def mix_kernel(layer, n_heads, part_ref, u_ref, gain_hbm, wo_hbm, wg_hbm, wu_hbm, wd_hbm, out_ref,
+def mix_kernel(layer, n_heads, n_next, part_ref, u_ref, gain_hbm, wo_hbm, wg_hbm, wu_hbm, wd_hbm, *rest):
+    next_src, out_ref, next_dst, rest = rest[:n_next], rest[n_next], rest[n_next + 1:2 * n_next + 1], rest[2 * n_next + 1:]
+    mix_body(layer, n_heads, part_ref, u_ref, gain_hbm, wo_hbm, wg_hbm, wu_hbm, wd_hbm, next_src, next_dst, out_ref, *rest)
+
+
+def mix_body(layer, n_heads, part_ref, u_ref, gain_hbm, wo_hbm, wg_hbm, wu_hbm, wd_hbm, next_src, next_dst, out_ref,
                wo_buf, wg_buf, wu_buf, wd_buf, core_in, fwd_out, fwd_in, y_out, y_in, u1_sc, h_out, h_in, hh, act,
                d_own, d_out, d_in, e_out, e_in, u_all, gain_ref, w_sem, send_sem, recv_sem):
     tp = lax.axis_index('tp')
@@ -209,7 +232,8 @@
         pltpu.make_async_copy(wd_hbm.at[layer, pl.ds(col0, ff), :], wd_buf, w_sem.at[3]),
         pltpu.make_async_copy(gain_hbm, gain_ref, w_sem.at[4]),
     ]
-    for cp in w_copies:
+    pre_copies = [pltpu.make_async_copy(src.at[layer + 1], dst, w_sem.at[5 + i]) for i, (src, dst) in enumerate(zip(next_src, next_dst))]
+    for cp in w_copies + pre_copies:
         cp.start()
 
     barrier = pltpu.get_barrier_semaphore()
@@ -308,44 +332,50 @@
         a_core[n].wait_recv()
         a_fwd[n].wait_recv()
         out_ref[:, n * width:(n + 1) * width] = u_all[n].astype(BF16)
+    for cp in pre_copies:
+        cp.wait()
     for cp in [c_far, c_own, fwd, h_copy] + y_copies + d_copies + e_copies + a_core + a_far + a_fwd:
         cp.wait_send()
 
 
-def mix(layer, part, u, gain, w_out, w_gate, w_up, w_down):
+def mix(layer, part, u, gain, w_out, w_gate, w_up, w_down, nxt):
     n_planes, n_rows, head_dim = part.shape
     n_heads = n_planes - 1
     d_model = u.shape[1]
     chunk = n_rows // 4
     n_tiles = w_gate.shape[2] // 128
     ff = ((n_tiles + 1) // 2) * 128
-    n_blk = 6
+    n_blk = 3
     width = d_model // n_blk
-    any_spec = pl.BlockSpec(memory_space=pltpu.HBM)
+    hbm = pl.BlockSpec(memory_space=pltpu.HBM)
     vm = pl.BlockSpec(memory_space=pltpu.VMEM)
     blocks = pltpu.VMEM((n_blk, chunk, width), F32)
     planes = pltpu.VMEM((n_planes, chunk, head_dim), F32)
     n_copies = 4 + 6 * n_blk
     return pl.pallas_call(
-        functools.partial(mix_kernel, layer, n_heads),
-        out_shape=jax.ShapeDtypeStruct((n_rows, d_model), BF16),
-        in_specs=[vm, vm] + [any_spec] * 5,
-        out_specs=vm,
+        functools.partial(mix_kernel, layer, n_heads, len(nxt)),
+        out_shape=[jax.ShapeDtypeStruct((n_rows, d_model), BF16)] + [pltpu.VMEM(w.shape[1:], w.dtype) for w in nxt],
+        in_specs=[vm, vm] + [hbm] * (5 + len(nxt)),
+        out_specs=[vm] * (1 + len(nxt)),
         scratch_shapes=[
             pltpu.VMEM((w_out.shape[1], d_model), BF16), pltpu.VMEM((d_model, ff), BF16), pltpu.VMEM((d_model, ff), BF16), pltpu.VMEM((ff, d_model), BF16),
             pltpu.VMEM((2, n_planes, chunk, head_dim), F32), planes, planes,
             blocks, blocks, pltpu.VMEM((chunk, d_model), F32), pltpu.VMEM((chunk, d_model), F32), pltpu.VMEM((chunk, d_model), F32),
             pltpu.VMEM((2 * chunk, d_model), BF16), pltpu.VMEM((2 * chunk, ff), BF16),
             blocks, blocks, blocks, blocks, blocks, pltpu.VMEM((n_blk, n_rows, width), F32),
-            pltpu.VMEM(gain.shape, BF16), pltpu.SemaphoreType.DMA((5,)), pltpu.SemaphoreType.DMA((n_copies,)), pltpu.SemaphoreType.DMA((n_copies,)),
+            pltpu.VMEM(gain.shape, BF16), pltpu.SemaphoreType.DMA((5 + len(nxt),)), pltpu.SemaphoreType.DMA((n_copies,)), pltpu.SemaphoreType.DMA((n_copies,)),
         ],
-        compiler_params=pltpu.CompilerParams(collective_id=layer, has_side_effects=True, vmem_limit_bytes=MIX_VMEM),
+        compiler_params=pltpu.CompilerParams(collective_id=layer, has_side_effects=True, vmem_limit_bytes=32 * 1024 * 1024),
         name=f"mix{layer}",
-    )(part, u, gain, w_out, w_gate, w_up, w_down)
+    )(part, u, gain, w_out, w_gate, w_up, w_down, *nxt)
 
 
 def in_hbm(x):
     return pltpu.with_memory_space_constraint(x, pltpu.HBM)
+
+
+def in_vmem(x):
+    return pltpu.with_memory_space_constraint(x, pltpu.VMEM)
 
 
 def solution(mesh):
@@ -361,13 +391,13 @@
         u = tok_emb.reshape(n_rows, d_model)
         u, lengths, freq, gain_attn, gain_mlp, kc, vc = map(in_hbm, (u, lengths, freq, gain_attn, gain_mlp, kc, vc))
         w_query, w_key, w_value, w_out, w_gate, w_up, w_down = map(in_hbm, (w_query, w_key, w_value, w_out, w_gate, w_up, w_down))
-        prev = None
-        for layer in range(n_layers):
-            res = attention(layer, n_steps, lengths, u, gain_attn, freq, w_query, w_key, w_value, kc, vc, prev)
-            part, prev = res[0], res[1:3]
-            if layer == 0:
-                u = res[3]
-            u = mix(layer, part, u, gain_mlp, w_out, w_gate, w_up, w_down)
+        n_heads = w_query.shape[2] // head_dim
+        nxt = [kc, vc, w_query, w_key, w_value]
+        res = attention(0, n_steps, n_heads, lengths, u, gain_attn, (freq, w_query, w_key, w_value, kc, vc))
+        u, *loc = mix(0, res['part'], res['u_perm'], gain_mlp, w_out, w_gate, w_up, w_down, nxt)
+        res = attention(1, n_steps, n_heads, lengths, u, gain_attn, (res['cos'], res['sin'], res['ko'], res['vo'], *loc))
+        u, = mix(1, res['part'], u, gain_mlp, w_out, w_gate, w_up, w_down, [])
+        prev = (res['ko'], res['vo'])
         hidden = u.reshape(n_batch, n_steps, d_model).transpose(1, 0, 2)
         return hidden, prev[0].reshape(key_cache.shape), prev[1].reshape(val_cache.shape)
 

time: 92.8 us -> 88.7 us (0.956)
  Pallas kernels: 91.1 us -> 87 us
    pallas_call x4, Pallas kernels: 91.1 us -> 87 us  [the longest x2 63.4 us: mix(): pl.pallas_call(functools.partial(mix_kernel, layer, n_heads, len(nxt)), o...]
where the time goes in v4:
time: 88.7 us; the launch traced here: 88.6 us
  Pallas kernels  87 us (98%)
  local copies, waits for them, and re-layouts  0.91 us (1%)
    pallas_call x2, Pallas kernels, mix(): pl.pallas_call(functools.partial(mix_kernel, layer, n_heads, len(nxt)), o...  63.4 us
    pallas_call x2, Pallas kernels, attention(): pl.pallas_call(functools.partial(attn_kernel, layer, n_steps, n_heads, na...  23.6 us

profile of v4, /device:TPU:0, one launch (start us, length us, event | category | flops | bytes accessed | tf_op | source)
XLA Modules:
  0.0 88.6 jit_solution(3221185347113994207)
XLA Ops:
  0.6 13.2 %attn0.1 = (f32[7,128,128]{2,1,0:T(8,128)S(1)}, bf16[2,32,1024,128]{3,2,1,0:T(8,128)(2,1)}, bf16[2,32,1024,128]{3,2,1,0:T(8,128)(2,1)}, bf16[128,1536]{1,0:T(8,1...) custom-call(s32[32]{0:T(128)} %refs_0_.3, bf16[128,1536]{1,0:T(8,128)(2,1)} %bitcast.18, ...), custom_call_target="tpu_custom_call" | custom-call | tf_op jit(solution)/shard_map/attn0/pallas_call | solution.py:183
  13.9 32.6 %mix0.1 = (bf16[128,1536]{1,0:T(8,128)(2,1)S(1)}, bf16[32,1024,128]{2,1,0:T(8,128)(2,1)S(1)}, bf16[32,1024,128]{2,1,0:T(8,128)(2,1)S(1)}, bf16[1536,768]{1,0:T(8...) custom-call(f32[7,128,128]{2,1,0:T(8,128)S(1)} %get-tuple-element.18.part_ref, ...), custom_call_target="tpu_custom_call" | custom-call | tf_op jit(solution)/shard_map/mix0/pallas_call | solution.py:355
  46.5 10.3 %attn1.1 = (f32[7,128,128]{2,1,0:T(8,128)S(1)}, bf16[2,32,1024,128]{3,2,1,0:T(8,128)(2,1)}, bf16[2,32,1024,128]{3,2,1,0:T(8,128)(2,1)}, bf16[32,1024,128]{2,1,0:T(8,128)(2,1)S(1)}, bf16[32,1024,128]{2,1,0:T(8,128)(2,1)S(1)}) custom-call(s32[32]{0:T(128)} %refs_0_.3, ...), custom_call_target="tpu_custom_call", output_to_operand_aliasing={{1}: (8, {}), {2}: (9, {}), {3}: (10, {}), {4}: (11, {})} | custom-call | tf_op jit(solution)/shard_map/attn1/pallas_call | solution.py:183
  56.9 30.8 %mix1.1 = bf16[128,1536]{1,0:T(8,128)(2,1)S(1)} custom-call(f32[7,128,128]{2,1,0:T(8,128)S(1)} %get-tuple-element.30.part_ref, bf16[128,1536]{1,0:T(8,128)(2,1)S(1)} %get-tuple-element.20.refs_1_.u_ref, bf16[2,1536]{1,0:T(2,128)(2,1)} %gain_hbm.3, bf16[2,768,1536]{2,1,0:T(8,128)(2,1)} %wo_hbm.3, bf16[2,1536,4480]{2,1,0:T(8,128)(2,1)} %wg_hbm.3, ...), custom_call_target="tpu_custom_call" | custom-call | tf_op jit(solution)/shard_map/mix1/pallas_call | solution.py:355
  87.7 0.1 reshape.27
  87.8 0.8 copy.25
